TPU v7x, 32 devices: a whole 2x2x4 slice. The times are simulated.
32 devices in a mesh: rep: 2 (over x), exp: 4 (over z), ten: 4 (over y, core).
Axes of the slice: x: 2, y: 2, z: 4, core: 2. Of those that a mesh axis runs over, the one named last changes fastest.
Arguments:
- hidden_in: bfloat16 [768, 3072], P(('rep', 'exp', 'ten')), parts along dimension 0, may hold values from -6 to 6
- queries: bfloat16 [768, 6144], P(('rep', 'exp', 'ten')), parts along dimension 0, may hold values from -100 to 100
- new_kv: bfloat16 [2, 768, 1024], P(None, ('rep', 'exp', 'ten')), parts along dimension 1, may hold values from -5 to 5
- prefix_kv: bfloat16 [2, 8, 128, 1024], P(None, ('rep', 'exp'), 'ten'), parts along dimension 1, may hold values from -5 to 5
- decode_kv: bfloat16 [2, 128, 48, 1024], P(None, ('rep', 'exp', 'ten')), parts along dimension 1, may hold values from -5 to 5
- prefix_len: int32 [8], P(('rep', 'exp')), parts along dimension 0, may hold values from 2 to 128
- decode_len: int32 [128], P(('rep', 'exp', 'ten')), parts along dimension 0, may hold values from 2 to 48
- out_proj: bfloat16 [6144, 3072], P('ten'), may hold values from -0.078125 to 0.078125
- norm_gain: float32 [3072], replicated, may hold values from 0.5 to 1.5
- router_w: bfloat16 [3072, 8], replicated, may hold values from -0.109375 to 0.109375
- expert_ids: int32 [768, 2], P(('rep', 'exp', 'ten')), parts along dimension 0, may hold values from 0 to 7, all different within a row; in each aligned block of 24 rows (0 to 23, 24 to 47, ...) at most 7 rows name the same one
- w_gate: bfloat16 [8, 3072, 8192], P('exp', None, 'ten'), may hold values from -0.109375 to 0.109375
- w_up: bfloat16 [8, 3072, 8192], P('exp', None, 'ten'), may hold values from -0.109375 to 0.109375
- w_down: bfloat16 [8, 8192, 3072], P('exp', 'ten'), may hold values from -0.0625 to 0.0625
Outputs:
- layer_out: bfloat16 [768, 3072], P(('rep', 'exp', 'ten')), parts along dimension 0
There are 2 independent parts, one for each index of `rep`. A program takes and returns all parts, laid end to end along the dimension named above; an argument that names none is the same for every part. Nothing has to cross between parts.
Inputs may be any that keep to these rules, and one draw needn't show every extreme that they name: `expert_ids`: each row names two different experts. Within each aligned block of 24 rows (the rows of one device) no expert is named by more than 7 rows, and in some block one expert is named by exactly 7 rows.
All inputs are finite; a program needn't handle non-finite values.
Results may differ from a plain program's by a relative error of at most 0.013.
Values may be sent and summed in bfloat16 or wider, within the bound.
No kernel may reach another device: no remote copies, remote signals or barrier semaphores. Data moves between devices by JAX's collectives and lax.ppermute only.
A program may use at most 128 MiB of HBM per device.

v0:
```python
import functools

import jax
import jax.numpy as jnp
from jax import lax
from jax.experimental import pallas as pl
from jax.experimental.pallas import tpu as pltpu
from jax.sharding import PartitionSpec as P

HD = 128
SLOTS = 8
F32 = jnp.float32
BF16 = jnp.bfloat16
MIB = 2**20
VMEM = pl.BlockSpec(memory_space=pltpu.VMEM)
SMEM = pl.BlockSpec(memory_space=pltpu.SMEM)
HBM = pl.BlockSpec(memory_space=pltpu.HBM)


def xor_pairs(size, distance):
    return [(i, i ^ distance) for i in range(size)]


def bit_reversed(size):
    order = [0]
    step = size // 2
    while step:
        order = order + [o + step for o in order]
        step //= 2
    return order


def up_bits(size):
    return [1 << b for b in range(size.bit_length() - 1)]


def out(shape, dtype):
    return jax.ShapeDtypeStruct(shape, dtype)


def held(array):
    return pltpu.with_memory_space_constraint(array, pltpu.VMEM)


def call(kernel, args, specs, outs, scratch=(), limit=4, flops=0, aliases=None):
    limit *= max(1, lax.axis_size("ten") * lax.axis_size("exp") // 16)
    args = [
        pltpu.with_memory_space_constraint(a, pltpu.HBM) if s is HBM else a
        for a, s in zip(args, specs)
    ]
    return pl.pallas_call(
        kernel,
        in_specs=specs,
        out_specs=[VMEM] * len(outs),
        out_shape=outs,
        scratch_shapes=list(scratch),
        compiler_params=pltpu.CompilerParams(vmem_limit_bytes=limit * MIB),
        cost_estimate=pl.CostEstimate(flops=flops, bytes_accessed=0, transcendentals=0),
        input_output_aliases=aliases or {},
    )(*args)


def load_all(pairs, sems):
    copies = [pltpu.make_async_copy(a, b, sems.at[i]) for i, (a, b) in enumerate(pairs)]
    for copy in copies:
        copy.start()
    return copies


def pack_kernel(q_hbm, new_hbm, prefix_hbm, *refs, heads_own, per_kv, kv_own):
    out_refs, (q_ref, new_ref, prefix_ref, sems) = refs[:-4], refs[-4:]
    pairs = ((q_hbm, q_ref), (new_hbm, new_ref), (prefix_hbm, prefix_ref))
    for copy in load_all(pairs, sems):
        copy.wait()
    me = lax.axis_index("ten")
    rows = q_ref.shape[0]
    prefix_rows = prefix_ref.shape[2]
    width = kv_own * HD
    pieces = heads_own // kv_own
    for d, out in enumerate(out_refs):
        t = me ^ d
        q_start = pl.multiple_of(t * (heads_own * HD), HD)
        for j in range(pieces):
            out[j * rows : (j + 1) * rows, :] = q_ref[
                :, pl.ds(pl.multiple_of(q_start + j * width, HD), width)
            ]
        kv_start = pl.multiple_of(((t * heads_own) // per_kv) * HD, HD)
        base = pieces * rows
        for s in range(2):
            out[base : base + rows, :] = new_ref[s, :, pl.ds(kv_start, width)]
            base += rows
        for s in range(2):
            out[base : base + prefix_rows, :] = prefix_ref[s, 0, :, pl.ds(kv_start, width)]
            base += prefix_rows


def decode_kernel(len_ref, q_ref, kv_hbm, new_hbm, *refs, per_kv, span_dev):
    out_refs, (kv_ref, new_ref, scratch, sems) = refs[:-4], refs[-4:]
    for copy in load_all(((kv_hbm, kv_ref), (new_hbm, new_ref)), sems):
        copy.wait()
    me = lax.axis_index("ten")
    dec_dev, ctx_len, kv_width = kv_ref.shape[1:]
    heads = q_ref.shape[0] // dec_dev
    heads_kv = kv_width // HD
    scale = HD ** (-0.5)
    row_group = lax.broadcasted_iota(jnp.int32, (heads, kv_width), 0) // per_kv
    lane_group = lax.broadcasted_iota(jnp.int32, (heads, kv_width), 1) // HD
    own = row_group == lane_group
    position = lax.broadcasted_iota(jnp.int32, (heads, ctx_len), 1)
    for r in range(dec_dev):
        q = q_ref[r * heads : (r + 1) * heads, :]
        wide = jnp.where(own, jnp.concatenate([q] * heads_kv, axis=1), jnp.zeros((), BF16))
        scores = (
            lax.dot_general(
                wide, kv_ref[0, r], (((1,), (1,)), ((), ())), preferred_element_type=F32
            )
            * scale
        )
        new_key = new_ref[0, span_dev + r : span_dev + r + 1, :].astype(F32)
        new_value = new_ref[1, span_dev + r : span_dev + r + 1, :].astype(F32)
        new_score = jnp.sum(wide.astype(F32) * new_key, axis=1, keepdims=True) * scale
        visible = position < len_ref[r]
        masked = jnp.where(visible, scores, -1e30)
        top = jnp.maximum(jnp.max(masked, axis=1, keepdims=True), new_score)
        exponent = jnp.where(visible, jnp.exp(masked - top), 0.0)
        new_exponent = jnp.exp(new_score - top)
        total = jnp.sum(exponent, axis=1, keepdims=True) + new_exponent
        mixed = jnp.dot(exponent.astype(BF16), kv_ref[1, r], preferred_element_type=F32)
        mixed = mixed + new_exponent.astype(BF16).astype(F32) * new_value
        mixed = jnp.where(own, mixed, 0.0)
        picked = mixed[:, :HD]
        for g in range(1, heads_kv):
            picked = picked + mixed[:, g * HD : (g + 1) * HD]
        scratch[pl.ds(r, heads, stride=dec_dev), :] = picked / total
    chunk = scratch.shape[0] // len(out_refs)
    for d, out in enumerate(out_refs):
        out[...] = scratch[pl.ds(pl.multiple_of((me ^ d) * chunk, 4), chunk), :].astype(BF16)


def attend_kernel(len_ref, *refs, ten, rows, prefix_rows, span_dev, heads_own, kv_own):
    packed, decoded = refs[:ten], refs[ten : 2 * ten]
    w_ref, ahead_ref, _ = refs[2 * ten : 2 * ten + 3]
    keep_ref, send_ref, ahead_out, att, sem = refs[2 * ten + 3 :]
    copy = pltpu.make_async_copy(ahead_ref.at[0], ahead_out, sem)
    copy.start()
    me = lax.axis_index("ten")
    dec_dev = rows - span_dev
    pieces = heads_own // kv_own
    scale = HD ** (-0.5)
    order = bit_reversed(ten)
    keys = ten * (prefix_rows + rows)
    prefix_keys = ten * prefix_rows
    all_rows = ten * rows
    row = lax.broadcasted_iota(jnp.int32, (all_rows, 1), 0)
    col = lax.broadcasted_iota(jnp.int32, (1, keys), 1)
    row_pos = jnp.zeros((all_rows, 1), jnp.int32)
    prefix_pos = jnp.full((1, keys), 1 << 30, jnp.int32)
    fresh_pos = jnp.full((1, keys), 1 << 30, jnp.int32)
    for b, d in enumerate(order):
        t = me ^ d
        i = row - b * rows
        row_pos = jnp.where((i >= 0) & (i < rows), t * span_dev + i, row_pos)
        p = col - b * prefix_rows
        prefix_pos = jnp.where((p >= 0) & (p < prefix_rows), t * prefix_rows + p, prefix_pos)
        f = col - prefix_keys - b * rows
        fresh_pos = jnp.where((f >= 0) & (f < span_dev), t * span_dev + f, fresh_pos)
    visible = (prefix_pos < len_ref[0]) | (fresh_pos <= row_pos)
    bias = jnp.where(visible, 0.0, -1e30)
    bias = jnp.concatenate([bias] * pieces, axis=0)
    new_base = pieces * rows
    prefix_base = new_base + 2 * rows
    for g in range(kv_own):
        lanes = slice(g * HD, (g + 1) * HD)

        def gather(s):
            start = prefix_base + s * prefix_rows
            fresh = new_base + s * rows
            return jnp.concatenate(
                [packed[d][start : start + prefix_rows, lanes] for d in order]
                + [packed[d][fresh : fresh + rows, lanes] for d in order],
                axis=0,
            )

        heads = range(g * pieces, (g + 1) * pieces)
        q = jnp.concatenate(
            [
                packed[d][
                    (h // kv_own) * rows : (h // kv_own + 1) * rows,
                    (h % kv_own) * HD : (h % kv_own + 1) * HD,
                ]
                for h in heads
                for d in order
            ],
            axis=0,
        )
        scores = (
            lax.dot_general(q, gather(0), (((1,), (1,)), ((), ())), preferred_element_type=F32)
            * scale
            + bias
        )
        top = jnp.max(scores, axis=1, keepdims=True)
        exponent = jnp.exp(scores - top)
        total = jnp.sum(exponent, axis=1, keepdims=True)
        out = jnp.dot(exponent.astype(BF16), gather(1), preferred_element_type=F32) / total
        for n, h in enumerate(heads):
            att[:, h * HD : (h + 1) * HD] = out[n * all_rows : (n + 1) * all_rows]
            for b, d in enumerate(order):
                att[b * rows + span_dev : (b + 1) * rows, h * HD : (h + 1) * HD] = decoded[d][
                    h * dec_dev : (h + 1) * dec_dev, :
                ].astype(F32)
    half = all_rows // 2
    attended = att[...].astype(BF16)
    step = 512
    for n in range(0, w_ref.shape[1], step):
        part = jnp.dot(attended, w_ref[:, n : n + step], preferred_element_type=F32)
        keep_ref[:, n : n + step] = part[:half]
        send_ref[:, n : n + step] = part[half:].astype(BF16)
    copy.wait()


def route_kernel(*refs, parts, groups, local, rows):
    addends = refs[:parts]
    hidden_ref, gain_ref, router_ref, ids_ref, _ = refs[parts : parts + 5]
    residual_ref, map_ref = refs[parts + 5 : parts + 7]
    slot_refs = refs[parts + 7 :]
    me = lax.axis_index("exp")
    residual = hidden_ref[...].astype(F32)
    for a in addends:
        residual = residual + a[:rows, :].astype(F32)
    residual_ref[...] = residual
    width = residual.shape[1]
    mean_square = jnp.sum(residual * residual, axis=1, keepdims=True) / width
    normed = (residual * lax.rsqrt(mean_square + 1e-05) * gain_ref[...]).astype(BF16)
    logits = lax.dot_general(
        normed, router_ref[...], (((1,), (1,)), ((), ())), preferred_element_type=F32
    )
    diagonal = lax.broadcasted_iota(jnp.int32, (rows, rows), 0) == lax.broadcasted_iota(
        jnp.int32, (rows, rows), 1
    )
    first, second = (
        jnp.sum(jnp.where(diagonal, ids_ref[k : k + 1, :], 0), axis=1, keepdims=True)
        for k in range(2)
    )
    expert = lax.broadcasted_iota(jnp.int32, logits.shape, 1)
    first_logit = jnp.sum(jnp.where(expert == first, logits, 0.0), axis=1, keepdims=True)
    second_logit = jnp.sum(jnp.where(expert == second, logits, 0.0), axis=1, keepdims=True)
    top = jnp.maximum(first_logit, second_logit)
    first_exp, second_exp = jnp.exp(first_logit - top), jnp.exp(second_logit - top)
    total = first_exp + second_exp
    slots = local * groups * SLOTS
    lane = lax.broadcasted_iota(jnp.int32, (rows, slots), 1)
    within = lane % SLOTS
    group = lane // (SLOTS * local)
    slot_expert = (group ^ me) * local + (lane // SLOTS) % local
    is_first, is_second = slot_expert == first, slot_expert == second
    named = is_first | is_second
    below = (
        lax.broadcasted_iota(jnp.int32, (rows, rows), 1)
        < lax.broadcasted_iota(jnp.int32, (rows, rows), 0)
    )
    rank = jnp.dot(
        jnp.where(below, 1.0, 0.0).astype(BF16),
        jnp.where(named, 1.0, 0.0).astype(BF16),
        preferred_element_type=F32,
    )
    placed = named & (rank == within.astype(F32))
    map_ref[...] = jnp.where(
        placed, jnp.where(is_first, first_exp / total, second_exp / total), 0.0
    )
    chosen = lax.dot_general(
        jnp.where(placed, 1.0, 0.0).astype(BF16),
        normed,
        (((0,), (0,)), ((), ())),
        preferred_element_type=F32,
    ).astype(BF16)
    block = local * SLOTS
    for s, out in enumerate(slot_refs):
        out[...] = chosen[s * block : (s + 1) * block, :]


def hidden_kernel(*refs, pieces, expert, tile, resident, last):
    xs, refs = refs[:pieces], refs[pieces:]
    if resident:
        gate_ref, up_ref, refs = refs[0], refs[1], refs[2:]
    else:
        gate_low, gate_high, up_low, up_hbm, down_hbm = refs[:5]
        refs = refs[5:]
    if not last:
        next_gate, refs = refs[0], refs[1:]
    hidden_ref, refs = refs[0], refs[1:]
    if not resident:
        up_rest, down_low, refs = refs[0], refs[1], refs[2:]
    if not last:
        next_low, refs = refs[0], refs[1:]
    x_all, sems = refs
    pending = []

    def start(source, target, n):
        pending.append(pltpu.make_async_copy(source, target, sems.at[n]))
        pending[-1].start()

    tiles = hidden_ref.shape[1] // tile
    up_copies = []
    if not resident:
        for i in range(1, tiles):
            up_copies.append(
                pltpu.make_async_copy(
                    up_hbm.at[expert, :, pl.ds(i * tile, tile)],
                    up_rest.at[:, pl.ds((i - 1) * tile, tile)],
                    sems.at[i],
                )
            )
            up_copies[-1].start()
    if not last:
        start(next_gate.at[expert + 1, :, pl.ds(0, next_low.shape[1])], next_low, 0)
    for i, p in enumerate(xs):
        x_all[i * SLOTS : (i + 1) * SLOTS, :] = p[expert * SLOTS : (expert + 1) * SLOTS, :]
    for i in range(tiles):
        cols = slice(i * tile, (i + 1) * tile)
        if resident:
            gate_tile = gate_ref[:, cols]
        else:
            gate_tile = gate_low[:, cols] if i < tiles - 1 else gate_high[...]
        gate = jnp.dot(x_all[...], gate_tile, preferred_element_type=F32)
        if resident:
            up_tile = up_ref[:, cols]
        elif i == 0:
            up_tile = up_low[...]
        else:
            up_copies[i - 1].wait()
            if i == tiles - 1:
                start(down_hbm.at[expert, :, pl.ds(0, down_low.shape[1])], down_low, tiles)
            up_tile = up_rest[:, (i - 1) * tile : i * tile]
        up = jnp.dot(x_all[...], up_tile, preferred_element_type=F32)
        hidden_ref[:, cols] = (gate / (1.0 + jnp.exp(-gate)) * up).astype(BF16)
    for copy in pending:
        copy.wait()


def down_kernel(hidden_ref, down_ref, *refs, resident, last, expert, tile, extra):
    if not resident:
        down_hbm, refs = refs[0], refs[1 + extra :]
    if not last:
        next_gate, next_up, refs = refs[0], refs[1], refs[2:]
    keep_ref, send_ref, refs = refs[0], refs[1], refs[2:]
    if not resident:
        rest_ref, refs = refs[0], refs[1:]
    if not last:
        gate_high, up_low, refs = refs[0], refs[1], refs[2:]
    sems = refs[0]
    split = down_ref.shape[1]
    half, width = keep_ref.shape
    pending = []
    if not last:
        low = next_gate.shape[2] - tile
        pending = load_all(
            (
                (next_gate.at[expert + 1, :, pl.ds(low, tile)], gate_high),
                (next_up.at[expert + 1, :, pl.ds(0, tile)], up_low),
            ),
            sems,
        )
    copies = []
    if not resident:
        for i in range((width - split) // tile):
            copies.append(
                pltpu.make_async_copy(
                    down_hbm.at[expert, :, pl.ds(split + i * tile, tile)],
                    rest_ref.at[:, pl.ds(i * tile, tile)],
                    sems.at[2 + i],
                )
            )
            copies[-1].start()
    for start in range(0, width, tile):
        cols = slice(start, start + tile)
        if start >= split:
            i = (start - split) // tile
            copies[i].wait()
            down_tile = rest_ref[:, i * tile : (i + 1) * tile]
        else:
            down_tile = down_ref[:, cols]
        part = jnp.dot(hidden_ref[...], down_tile, preferred_element_type=F32)
        keep_ref[:, cols] = part[:half]
        send_ref[:, cols] = part[half:].astype(BF16)
    for copy in pending:
        copy.wait()


def add_kernel(*refs, parts, first, rows, skip=0):
    addends, outs = refs[:parts], refs[parts + skip :]
    total = addends[0][first : first + rows, :].astype(F32)
    for a in addends[1:]:
        total = total + a[first : first + rows, :].astype(F32)
    each = outs[0].shape[0]
    for i, out in enumerate(outs):
        out[...] = total[i * each : (i + 1) * each, :].astype(out.dtype)


def mix_kernel(residual_ref, map_ref, *refs, local, groups):
    returned, out = refs[:-1], refs[-1]
    rows = residual_ref.shape[0]
    table = jnp.concatenate(
        [returned[e * groups + d][...] for d in range(groups) for e in range(local)], axis=0
    )
    weights = map_ref[...]
    high = weights.astype(BF16)
    rest = weights - high.astype(F32)
    middle = rest.astype(BF16)
    low = (rest - middle.astype(F32)).astype(BF16)
    stacked = jnp.concatenate([high, middle, low], axis=0)
    mixed = jnp.dot(stacked, table, preferred_element_type=F32)
    total = mixed[:rows] + mixed[rows : 2 * rows] + mixed[2 * rows :]
    out[...] = (residual_ref[...] + total).astype(out.dtype)


def fetch_kernel(source_ref, _, out_ref, token_ref, sem, *, expert):
    source = source_ref if expert is None else source_ref.at[expert]
    copy = pltpu.make_async_copy(source.at[:, pl.ds(0, out_ref.shape[1])], out_ref, sem)
    copy.start()
    token_ref[...] = jnp.zeros_like(token_ref)
    copy.wait()


def fetch(source, expert, after, columns=None):
    rows, width = source.shape[-2:]
    return call(
        functools.partial(fetch_kernel, expert=expert),
        (source, after),
        [HBM, VMEM],
        [out((rows, columns or width), BF16), out((8, HD), F32)],
        [pltpu.SemaphoreType.DMA],
        limit=2,
    )


def send_to(x, axis, distance):
    return lax.ppermute(x, axis, xor_pairs(lax.axis_size(axis), distance))


def halves_down(keep, send, axis, size):
    addends = [keep]
    rows = keep.shape[0]
    last_sent = send
    for bit in up_bits(size):
        addends.append(send_to(send, axis, bit))
        last_sent = send
        if bit * 2 < size:
            rows //= 2
            send = call(
                functools.partial(add_kernel, parts=len(addends), first=rows, rows=rows),
                addends,
                [VMEM] * len(addends),
                [out((rows, keep.shape[1]), BF16)],
                limit=3,
            )[0]
    return addends, rows, last_sent


def on_device(
    hidden_in,
    queries,
    new_kv,
    prefix_kv,
    decode_kv,
    prefix_len,
    decode_len,
    out_proj,
    norm_gain,
    router_w,
    expert_ids,
    w_gate,
    w_up,
    w_down,
):
    ten = lax.axis_size("ten")
    groups = lax.axis_size("exp")
    rows, width = hidden_in.shape
    dec_dev = decode_len.shape[0]
    span_dev = rows - dec_dev
    heads_q = queries.shape[1] // HD
    heads_kv = new_kv.shape[2] // HD
    per_kv = heads_q // heads_kv
    heads_own = heads_q // ten
    kv_own = max(1, heads_own // per_kv)
    prefix_rows = prefix_kv.shape[2]
    experts = router_w.shape[1]
    local = experts // groups

    packed_rows = (heads_own // kv_own) * rows + 2 * rows + 2 * prefix_rows
    packed = call(
        functools.partial(pack_kernel, heads_own=heads_own, per_kv=per_kv, kv_own=kv_own),
        (queries, new_kv, prefix_kv),
        [HBM] * 3,
        [out((packed_rows, kv_own * HD), BF16)] * ten,
        [pltpu.VMEM(a.shape, BF16) for a in (queries, new_kv, prefix_kv)]
        + [pltpu.SemaphoreType.DMA((3,))],
    )
    packed = [packed[0]] + [
        lax.ppermute(packed[d], "ten", xor_pairs(ten, d)) for d in range(1, ten)
    ]

    decoded = call(
        functools.partial(decode_kernel, per_kv=per_kv, span_dev=span_dev),
        (
            decode_len,
            queries[span_dev:].reshape(dec_dev * heads_q, HD),
            decode_kv,
            new_kv,
        ),
        [SMEM, VMEM, HBM, HBM],
        [out((heads_own * dec_dev, HD), BF16)] * ten,
        [
            pltpu.VMEM(decode_kv.shape, BF16),
            pltpu.VMEM(new_kv.shape, BF16),
            pltpu.VMEM((heads_q * dec_dev, HD), F32),
            pltpu.SemaphoreType.DMA((2,)),
        ],
        limit=4,
    )
    own_decoded = decoded[0]
    decoded = [decoded[0]] + [
        lax.ppermute(decoded[d], "ten", xor_pairs(ten, d)) for d in range(1, ten)
    ]
    proj, proj_token = fetch(out_proj, None, own_decoded)

    half = ten * rows // 2
    keep, send, up = call(
        functools.partial(
            attend_kernel,
            ten=ten,
            rows=rows,
            prefix_rows=prefix_rows,
            span_dev=span_dev,
            heads_own=heads_own,
            kv_own=kv_own,
        ),
        (prefix_len, *packed, *decoded, held(proj), w_up, proj_token),
        [SMEM] + [VMEM] * (2 * ten) + [VMEM, HBM, VMEM],
        [
            out((half, width), F32),
            out((half, width), BF16),
            out(w_up.shape[1:], BF16),
        ],
        [pltpu.VMEM((ten * rows, heads_own * HD), F32), pltpu.SemaphoreType.DMA],
        limit=4,
    )
    addends, _, last_sent = halves_down(keep, send, "ten", ten)
    down, down_token = fetch(w_down, 0, last_sent)

    routed = call(
        functools.partial(
            route_kernel, parts=len(addends), groups=groups, local=local, rows=rows
        ),
        (
            *addends,
            hidden_in,
            norm_gain.reshape(1, width),
            router_w.T,
            expert_ids.T,
            down_token,
        ),
        [VMEM] * (len(addends) + 5),
        [out((rows, width), F32), out((rows, experts * SLOTS), F32)]
        + [out((local * SLOTS, width), BF16)] * groups,
        limit=3,
    )
    residual, weight_map, slots = routed[0], routed[1], routed[2:]

    block = [slots[0]] + [send_to(slots[d], "exp", d) for d in range(1, groups)]
    for bit in reversed(up_bits(ten)):
        block = block + [send_to(b, "ten", bit) for b in block]

    gate, _ = fetch(w_gate, 0, slots[0])
    hidden_units = w_gate.shape[2]
    tile = min(512, hidden_units // 4)
    tiles = hidden_units // tile
    down_low_width = 2 * tile
    half = len(block) * SLOTS // 2
    returned = []
    for e in range(local):
        last, resident = e == local - 1, e == 0
        args, specs = [*block], [VMEM] * len(block)
        outs = [out((2 * half, hidden_units), BF16)]
        if resident:
            args += [held(gate), held(up)]
            specs += [VMEM] * 2
        else:
            args += [held(next_low), held(gate_high), held(up_low), w_up, w_down]
            specs += [VMEM] * 3 + [HBM] * 2
            outs += [
                out((width, hidden_units - tile), BF16),
                out((hidden_units, down_low_width), BF16),
            ]
        if not last:
            args.append(w_gate)
            specs.append(HBM)
            outs.append(out((width, hidden_units - tile), BF16))
        hidden, *rest = call(
            functools.partial(
                hidden_kernel,
                pieces=len(block),
                expert=e,
                tile=tile,
                resident=resident,
                last=last,
            ),
            args,
            specs,
            outs,
            [pltpu.VMEM((2 * half, width), BF16), pltpu.SemaphoreType.DMA((tiles + 1,))],
            limit=3,
            flops=8 * half * width * hidden_units,
        )
        if not last:
            next_low = rest[-1]
        args, specs = [hidden], [VMEM]
        outs = [out((half, width), F32), out((half, width), BF16)]
        if resident:
            args.append(held(down))
            specs.append(VMEM)
        else:
            args += [held(rest[1]), w_down, rest[0], before]
            specs += [VMEM, HBM, VMEM, VMEM]
            outs.append(out((hidden_units, width - down_low_width), BF16))
        if not last:
            args += [w_gate, w_up]
            specs += [HBM, HBM]
            outs += [out((width, tile), BF16)] * 2
        keep, send, *rest = call(
            functools.partial(
                down_kernel, resident=resident, last=last, expert=e, tile=tile, extra=2
            ),
            args,
            specs,
            outs,
            [pltpu.SemaphoreType.DMA((2 + width // tile,))],
            limit=3,
            flops=4 * half * width * hidden_units,
        )
        if not last:
            gate_high, up_low = rest[-2:]
            rest = rest[:-2]
        addends, share, before = halves_down(keep, send, "ten", ten)
        pieces = call(
            functools.partial(
                add_kernel, parts=len(addends), first=0, rows=share, skip=len(rest)
            ),
            (*addends, *rest),
            [VMEM] * (len(addends) + len(rest)),
            [out((SLOTS, width), BF16)] * groups,
            limit=3,
        )
        returned.append(pieces[0])
        returned += [
            lax.ppermute(pieces[d], "exp", xor_pairs(groups, d)) for d in range(1, groups)
        ]
    return pl.pallas_call(
        functools.partial(mix_kernel, local=local, groups=groups),
        in_specs=[VMEM] * (2 + len(returned)),
        out_specs=VMEM,
        out_shape=jax.ShapeDtypeStruct((rows, width), BF16),
        compiler_params=pltpu.CompilerParams(vmem_limit_bytes=16 * MIB),
        name="mix",
    )(residual, weight_map, *returned)


def solution(mesh):
    in_specs = (
        P(("rep", "exp", "ten"), None),
        P(("rep", "exp", "ten"), None),
        P(None, ("rep", "exp", "ten"), None),
        P(None, ("rep", "exp"), "ten", None),
        P(None, ("rep", "exp", "ten"), None, None),
        P(("rep", "exp")),
        P(("rep", "exp", "ten")),
        P("ten", None),
        P(),
        P(),
        P(("rep", "exp", "ten"), None),
        P("exp", None, "ten"),
        P("exp", None, "ten"),
        P("exp", "ten", None),
    )
    out_specs = P(("rep", "exp", "ten"), None)

    return jax.shard_map(
        on_device, mesh=mesh, in_specs=in_specs, out_specs=out_specs, check_vma=False
    )
```

profile of v0, /device:TPU:0, one launch (start us, length us, event | category | flops | bytes accessed | tf_op | source)
XLA Modules:
  0.0 95.9 jit_solution(5117699792983732138)
XLA Ops:
  0.0 1.1 %shard_map.136 = (bf16[256,256]{1,0:T(8,128)(2,1)S(1)}, bf16[256,256]{1,0:T(8,128)(2,1)S(1)}, bf16[256,256]{1,0:T(8,128)(2,1)S(1)}, bf16[256,256]{1,0:T(8,128)(2,1)S(1)}) custom-call(bf16[24,6144]{1,0:T(8,128)(2,1)} %q_hbm.1, bf16[2,24,1024]{2,1,0:T(8,128)(2,1)} %new_hbm.3, bf16[2,1,32,1024]{3,2,1,0:T(8,128)(2,1)} %prefix_hbm.1), custom_call_target="tpu_custom_call" | custom-call | tf_op jit(solution)/shard_map/pallas_call | solution.py:51
  1.1 0.6 collective-permute-start
  1.7 2.6 %collective-permute-start.1 = (bf16[256,256]{1,0:T(8,128)(2,1)S(1)}, bf16[256,256]{1,0:T(8,128)(2,1)S(1)}, u32[]{:S(2)}, u32[]{:S(2)}) collective-permute-start(bf16[256,256]{1,0:T(8,128)(2,1)S(1)} %get-tuple-element.49), channel_id=1, source_target_pairs={{0,2},{1,3},{2,0},{3,1},{4,6},{5,7},{6,4},{7,5},{8,10},{9,11},{10,... | collective-permute-start | bytes 393224 | tf_op jit(solution)/shard_map/ppermute | solution.py:499
  4.3 0.0 collective-permute-start.2
  4.3 0.9 slice.3
  5.3 0.0 copy-start.4
  5.3 0.6 copy-done.4
  5.9 2.5 %shard_map.137 = (bf16[48,128]{1,0:T(8,128)(2,1)S(1)}, bf16[48,128]{1,0:T(8,128)(2,1)S(1)}, bf16[48,128]{1,0:T(8,128)(2,1)S(1)}, bf16[48,128]{1,0:T(8,128)(2,1)S(1)}) custom-call(s32[4]{0:T(128)S(1)} %copy-done.4, bf16[192,128]{1,0:T(8,128)(2,1)S(1)} %reshape.6.q_ref, bf16[2,4,48,1024]{3,2,1,0:T(8,128)(2,1)} %kv_hbm.1, bf16[2,24,1024]{2,1,0:T(8,128)(2,1)} %new_hbm.3), custom_call_target="tpu_custom_call" | custom-call | tf_op jit(solution)/shard_map/pallas_call | solution.py:51
  8.5 0.2 collective-permute-start.3
  8.7 1.9 %collective-permute-start.4 = (bf16[48,128]{1,0:T(8,128)(2,1)S(1)}, bf16[48,128]{1,0:T(8,128)(2,1)S(1)}, u32[]{:S(2)}, u32[]{:S(2)}) collective-permute-start(bf16[48,128]{1,0:T(8,128)(2,1)S(1)} %get-tuple-element.53), channel_id=1, source_target_pairs={{0,2},{1,3},{2,0},{3,1},{4,6},{5,7},{6,4},{7,5},{8,10},{9,11},{10,... | collective-permute-start | bytes 36872 | tf_op jit(solution)/shard_map/ppermute | solution.py:522
  10.7 0.8 collective-permute-start.5
  12.1 3.7 %shard_map.138 = (bf16[1536,3072]{1,0:T(8,128)(2,1)S(1)}, f32[8,128]{1,0:T(8,128)S(1)}) custom-call(bf16[1536,3072]{1,0:T(8,128)(2,1)} %source_ref.3, bf16[48,128]{1,0:T(8,128)(2,1)S(1)} %get-tuple-element.51._.refs_4_), custom_call_target="tpu_custom_call" | custom-call | tf_op jit(solution)/shard_map/pallas_call | solution.py:51
  15.8 0.0 collective-permute-done.4.refs_6_
  15.8 0.0 collective-permute-done.refs_1_
  15.8 0.0 collective-permute-done.1.refs_2_
  15.8 4.6 %shard_map.139 = (f32[48,3072]{1,0:T(8,128)S(1)}, bf16[48,3072]{1,0:T(8,128)(2,1)S(1)}, bf16[3072,2048]{1,0:T(8,128)(2,1)S(1)}) custom-call(s32[1]{0:T(128)S(6)} %copy.15.len_ref, bf16[256,256]{1,0:T(8,128)(2,1)S(1)} %get-tuple-element.47.refs_0_, bf16[256,256]{1,0:T(8,128)(2,1)S(1)} %collective-permute-done.refs_1_, ...), custom_call_target="tpu_custom_call" | custom-call | tf_op jit(solution)/shard_map/pallas_call | solution.py:51
  20.4 0.2 collective-permute-start.6
  20.7 1.4 %collective-permute-done.6.refs_1_ = bf16[48,3072]{1,0:T(8,128)(2,1)S(1)} collective-permute-done((bf16[48,3072]{1,0:T(8,128)(2,1)S(1)}, bf16[48,3072]{1,0:T(8,128)(2,1)S(1)}, u32[]{:S(2)}, u32[]{:S(2)}) %collective-permute-start.6) | collective-permute-done | bytes 294944 | tf_op jit(solution)/shard_map/ppermute | solution.py:437
  22.1 0.0 copy-start
  22.1 0.0 copy-start.1
  22.2 0.0 copy-start.2
  22.2 0.0 copy-start.3
  22.2 1.1 %collective-permute-start.7 = (bf16[24,3072]{1,0:T(8,128)(2,1)S(1)}, bf16[24,3072]{1,0:T(8,128)(2,1)S(1)}, u32[]{:S(2)}, u32[]{:S(2)}) collective-permute-start(bf16[24,3072]{1,0:T(8,128)(2,1)S(1)} %shard_map.140._), channel_id=1, source_target_pairs={{0,2},{1,3},{2,0},{3,1},{4,6},{5,7},{6,4},{7,5},{8,10},{9,11},{10,... | collective-permute-start | bytes 442376 | tf_op jit(solution)/shard_map/ppermute | solution.py:437
  23.2 4.6 %shard_map.141 = (bf16[2048,3072]{1,0:T(8,128)(2,1)S(1)}, f32[8,128]{1,0:T(8,128)S(1)}) custom-call(bf16[2,2048,3072]{2,1,0:T(8,128)(2,1)} %refs_0_.3, bf16[24,3072]{1,0:T(8,128)(2,1)S(1)} %shard_map.140._), custom_call_target="tpu_custom_call" | custom-call | tf_op jit(solution)/shard_map/pallas_call | solution.py:51
  27.8 0.3 collective-permute-done.7.refs_2_
  28.2 0.6 shard_map.142
  28.7 1.6 %collective-permute-start.8 = (bf16[16,3072]{1,0:T(8,128)(2,1)S(1)}, bf16[16,3072]{1,0:T(8,128)(2,1)S(1)}, u32[]{:S(2)}, u32[]{:S(2)}) collective-permute-start(bf16[16,3072]{1,0:T(8,128)(2,1)S(1)} %get-tuple-element.63), channel_id=1, source_target_pairs={{0,4},{4,0},{8,12},{12,8},{1,5},{5,1},{9,13},{13,9},{2,6},{6,2},{1... | collective-permute-start | bytes 294920 | tf_op jit(solution)/shard_map/ppermute | solution.py:437
  30.4 2.6 %collective-permute-start.9 = (bf16[16,3072]{1,0:T(8,128)(2,1)S(1)}, bf16[16,3072]{1,0:T(8,128)(2,1)S(1)}, u32[]{:S(2)}, u32[]{:S(2)}) collective-permute-start(bf16[16,3072]{1,0:T(8,128)(2,1)S(1)} %get-tuple-element.64), channel_id=1, source_target_pairs={{0,8},{4,12},{8,0},{12,4},{1,9},{5,13},{9,1},{13,5},{2,10},{6,14},... | collective-permute-start | bytes 294920 | tf_op jit(solution)/shard_map/ppermute | solution.py:437
  33.0 0.2 collective-permute-start.10
  33.2 0.0 collective-permute-start.15
  33.2 1.2 %collective-permute-start.11 = (bf16[16,3072]{1,0:T(8,128)(2,1)S(1)}, bf16[16,3072]{1,0:T(8,128)(2,1)S(1)}, u32[]{:S(2)}, u32[]{:S(2)}) collective-permute-start(bf16[16,3072]{1,0:T(8,128)(2,1)S(1)} %get-tuple-element.62._.refs_0_), channel_id=1, source_target_pairs={{0,2},{1,3},{2,0},{3,1},{4,6},{5,7},{6,4},{7,5},{8,10},{9,11},{10,... | collective-permute-start | bytes 294920 | tf_op jit(solution)/shard_map/ppermute | solution.py:437
  34.4 0.0 collective-permute-done.8.refs_1_
  34.4 0.2 collective-permute-start.16
  34.6 6.1 %collective-permute-done.9.refs_2_ = bf16[16,3072]{1,0:T(8,128)(2,1)S(1)} collective-permute-done((bf16[16,3072]{1,0:T(8,128)(2,1)S(1)}, bf16[16,3072]{1,0:T(8,128)(2,1)S(1)}, u32[]{:S(2)}, u32[]{:S(2)}) %collective-permute-start.9) | collective-permute-done | bytes 98336 | tf_op jit(solution)/shard_map/ppermute | solution.py:437
  40.8 0.9 collective-permute-start.12
  41.7 1.2 %collective-permute-start.13 = (bf16[16,3072]{1,0:T(8,128)(2,1)S(1)}, bf16[16,3072]{1,0:T(8,128)(2,1)S(1)}, u32[]{:S(2)}, u32[]{:S(2)}) collective-permute-start(bf16[16,3072]{1,0:T(8,128)(2,1)S(1)} %collective-permute-done.9.refs_2_), channel_id=1, source_target_pairs={{0,2},{1,3},{2,0},{3,1},{4,6},{5,7},{6,4},{7,5},{8,10},{9,11},{10,... | collective-permute-start | bytes 294920 | tf_op jit(solution)/shard_map/ppermute | solution.py:437
  42.9 0.9 collective-permute-start.14
  43.8 2.1 %collective-permute-done.12.refs_5_ = bf16[16,3072]{1,0:T(8,128)(2,1)S(1)} collective-permute-done((bf16[16,3072]{1,0:T(8,128)(2,1)S(1)}, bf16[16,3072]{1,0:T(8,128)(2,1)S(1)}, u32[]{:S(2)}, u32[]{:S(2)}) %collective-permute-start.12) | collective-permute-done | bytes 98336 | tf_op jit(solution)/shard_map/ppermute | solution.py:437
  46.0 0.5 collective-permute-start.20
  46.5 1.6 %collective-permute-done.13.refs_6_ = bf16[16,3072]{1,0:T(8,128)(2,1)S(1)} collective-permute-done((bf16[16,3072]{1,0:T(8,128)(2,1)S(1)}, bf16[16,3072]{1,0:T(8,128)(2,1)S(1)}, u32[]{:S(2)}, u32[]{:S(2)}) %collective-permute-start.13) | collective-permute-done | bytes 98336 | tf_op jit(solution)/shard_map/ppermute | solution.py:437
  48.1 1.5 %collective-permute-done.14.refs_7_ = bf16[16,3072]{1,0:T(8,128)(2,1)S(1)} collective-permute-done((bf16[16,3072]{1,0:T(8,128)(2,1)S(1)}, bf16[16,3072]{1,0:T(8,128)(2,1)S(1)}, u32[]{:S(2)}, u32[]{:S(2)}) %collective-permute-start.14) | collective-permute-done | bytes 98336 | tf_op jit(solution)/shard_map/ppermute | solution.py:437
  49.6 5.2 %shard_map.143 = (bf16[3072,2048]{1,0:T(8,128)(2,1)S(1)}, f32[8,128]{1,0:T(8,128)}) custom-call(bf16[2,3072,2048]{2,1,0:T(8,128)(2,1)} %refs_0_.2, bf16[16,3072]{1,0:T(8,128)(2,1)S(1)} %get-tuple-element.62._.refs_0_), custom_call_target="tpu_custom_call" | custom-call | tf_op jit(solution)/shard_map/pallas_call | solution.py:51
  54.8 4.2 %shard_map.144 = (bf16[128,2048]{1,0:T(8,128)(2,1)S(1)}, bf16[3072,1536]{1,0:T(8,128)(2,1)S(1)}) custom-call(bf16[16,3072]{1,0:T(8,128)(2,1)S(1)} %get-tuple-element.62._.refs_0_, bf16[16,3072]{1,0:T(8,128)(2,1)S(1)} %collective-permute-done.8.refs_1_, bf16[16,3072]{1,0:T(8,128)(2,1)S(1)} %collective-permute-done.9.refs_2_, ...), custom_call_target="tpu_custom_call" | custom-call | flops 3221225472 | tf_op jit(solution)/shard_map/pallas_call | solution.py:51
  59.0 3.0 %shard_map.145 = (f32[64,3072]{1,0:T(8,128)S(1)}, bf16[64,3072]{1,0:T(8,128)(2,1)S(1)}, bf16[3072,512]{1,0:T(8,128)(2,1)S(1)}, bf16[3072,512]{1,0:T(8,128)(2,1)S(1)}) custom-call(bf16[128,2048]{1,0:T(8,128)(2,1)S(1)} %get-tuple-element.68.hidden_ref, bf16[2048,3072]{1,0:T(8,128)(2,1)S(1)} %get-tuple-element.69.down_ref, bf16[2,3072,2048]{2,1,0:T(8,128)(2,1)} %refs_0_.2, ...), custom_call_target="tpu_custom_call" | custom-call | flops 1610612736 | tf_op jit(solution)/shard_map/pallas_call | solution.py:51
  62.0 0.6 collective-permute-start.23
  62.6 6.8 %shard_map.148 = (bf16[128,2048]{1,0:T(8,128)(2,1)S(1)}, bf16[3072,1536]{1,0:T(8,128)(2,1)S(1)}, bf16[2048,1024]{1,0:T(8,128)(2,1)S(1)}) custom-call(bf16[16,3072]{1,0:T(8,128)(2,1)S(1)} %get-tuple-element.62._.refs_0_, bf16[16,3072]{1,0:T(8,128)(2,1)S(1)} %collective-permute-done.8.refs_1_, bf16[16,3072]{1,0:T(8,128)(2,1)S(1)} %collective-permute-done.9.refs_2_, ...), custom_call_target="tpu_custom_call" | custom-call | flops 3221225472 | tf_op jit(solution)/shard_map/pallas_call | solution.py:51
  69.4 4.1 %shard_map.149 = (f32[64,3072]{1,0:T(8,128)S(1)}, bf16[64,3072]{1,0:T(8,128)(2,1)S(1)}, bf16[2048,2048]{1,0:T(8,128)(2,1)S(1)}) custom-call(bf16[128,2048]{1,0:T(8,128)(2,1)S(1)} %get-tuple-element.79.hidden_ref, bf16[2048,1024]{1,0:T(8,128)(2,1)S(1)} %get-tuple-element.80.down_ref, bf16[2,2048,3072]{2,1,0:T(8,128)(2,1)} %refs_0_.3, ...), custom_call_target="tpu_custom_call" | custom-call | flops 1610612736 | tf_op jit(solution)/shard_map/pallas_call | solution.py:51
  73.5 0.1 collective-permute-start.28
  73.6 1.0 %collective-permute-start.24 = (bf16[32,3072]{1,0:T(8,128)(2,1)S(1)}, bf16[32,3072]{1,0:T(8,128)(2,1)S(1)}, u32[]{:S(2)}, u32[]{:S(2)}) collective-permute-start(bf16[32,3072]{1,0:T(8,128)(2,1)S(1)} %shard_map.146.refs_2_), channel_id=1, source_target_pairs={{0,2},{1,3},{2,0},{3,1},{4,6},{5,7},{6,4},{7,5},{8,10},{9,11},{10,... | collective-permute-start | bytes 589832 | tf_op jit(solution)/shard_map/ppermute | solution.py:437
  74.6 0.7 collective-permute-done.28.refs_1_
  75.3 1.0 %collective-permute-start.29 = (bf16[32,3072]{1,0:T(8,128)(2,1)S(1)}, bf16[32,3072]{1,0:T(8,128)(2,1)S(1)}, u32[]{:S(2)}, u32[]{:S(2)}) collective-permute-start(bf16[32,3072]{1,0:T(8,128)(2,1)S(1)} %shard_map.150), channel_id=1, source_target_pairs={{0,2},{1,3},{2,0},{3,1},{4,6},{5,7},{6,4},{7,5},{8,10},{9,11},{10,... | collective-permute-start | bytes 589832 | tf_op jit(solution)/shard_map/ppermute | solution.py:437
  76.3 5.1 %collective-permute-done.24.refs_2_ = bf16[32,3072]{1,0:T(8,128)(2,1)S(1)} collective-permute-done((bf16[32,3072]{1,0:T(8,128)(2,1)S(1)}, bf16[32,3072]{1,0:T(8,128)(2,1)S(1)}, u32[]{:S(2)}, u32[]{:S(2)}) %collective-permute-start.24) | collective-permute-done | bytes 196640 | tf_op jit(solution)/shard_map/ppermute | solution.py:437
  81.4 0.1 shard_map.147
  81.5 0.2 collective-permute-start.25
  81.7 2.9 %collective-permute-start.26 = (bf16[8,3072]{1,0:T(8,128)(2,1)S(1)}, bf16[8,3072]{1,0:T(8,128)(2,1)S(1)}, u32[]{:S(2)}, u32[]{:S(2)}) collective-permute-start(bf16[8,3072]{1,0:T(8,128)(2,1)S(1)} %get-tuple-element.74), channel_id=1, source_target_pairs={{0,8},{4,12},{8,0},{12,4},{1,9},{5,13},{9,1},{13,5},{2,10},{6,14},... | collective-permute-start | bytes 147464 | tf_op jit(solution)/shard_map/ppermute | solution.py:655
  84.6 1.4 %collective-permute-start.27 = (bf16[8,3072]{1,0:T(8,128)(2,1)S(1)}, bf16[8,3072]{1,0:T(8,128)(2,1)S(1)}, u32[]{:S(2)}, u32[]{:S(2)}) collective-permute-start(bf16[8,3072]{1,0:T(8,128)(2,1)S(1)} %get-tuple-element.75), channel_id=1, source_target_pairs={{0,12},{4,8},{8,4},{12,0},{1,13},{5,9},{9,5},{13,1},{2,14},{6,10},... | collective-permute-start | bytes 147464 | tf_op jit(solution)/shard_map/ppermute | solution.py:655
  85.9 0.1 shard_map.151
  86.0 0.1 collective-permute-start.30
  86.1 3.0 %collective-permute-start.31 = (bf16[8,3072]{1,0:T(8,128)(2,1)S(1)}, bf16[8,3072]{1,0:T(8,128)(2,1)S(1)}, u32[]{:S(2)}, u32[]{:S(2)}) collective-permute-start(bf16[8,3072]{1,0:T(8,128)(2,1)S(1)} %get-tuple-element.87), channel_id=1, source_target_pairs={{0,8},{4,12},{8,0},{12,4},{1,9},{5,13},{9,1},{13,5},{2,10},{6,14},... | collective-permute-start | bytes 147464 | tf_op jit(solution)/shard_map/ppermute | solution.py:655
  89.1 1.4 %collective-permute-start.32 = (bf16[8,3072]{1,0:T(8,128)(2,1)S(1)}, bf16[8,3072]{1,0:T(8,128)(2,1)S(1)}, u32[]{:S(2)}, u32[]{:S(2)}) collective-permute-start(bf16[8,3072]{1,0:T(8,128)(2,1)S(1)} %get-tuple-element.88), channel_id=1, source_target_pairs={{0,12},{4,8},{8,4},{12,0},{1,13},{5,9},{9,5},{13,1},{2,14},{6,10},... | collective-permute-start | bytes 147464 | tf_op jit(solution)/shard_map/ppermute | solution.py:655
  90.5 0.2 collective-permute-done.27.refs_3_
  90.7 1.0 %collective-permute-done.31.refs_6_ = bf16[8,3072]{1,0:T(8,128)(2,1)S(1)} collective-permute-done((bf16[8,3072]{1,0:T(8,128)(2,1)S(1)}, bf16[8,3072]{1,0:T(8,128)(2,1)S(1)}, u32[]{:S(2)}, u32[]{:S(2)}) %collective-permute-start.31) | collective-permute-done | bytes 49184 | tf_op jit(solution)/shard_map/ppermute | solution.py:655
  91.7 3.3 %collective-permute-done.32.refs_7_ = bf16[8,3072]{1,0:T(8,128)(2,1)S(1)} collective-permute-done((bf16[8,3072]{1,0:T(8,128)(2,1)S(1)}, bf16[8,3072]{1,0:T(8,128)(2,1)S(1)}, u32[]{:S(2)}, u32[]{:S(2)}) %collective-permute-start.32) | collective-permute-done | bytes 49184 | tf_op jit(solution)/shard_map/ppermute | solution.py:655
  95.0 0.9 mix.1
  (31 shorter events, 0.2 us)
Async XLA Ops:
  1.1 14.7 %collective-permute-start = (bf16[256,256]{1,0:T(8,128)(2,1)S(1)}, bf16[256,256]{1,0:T(8,128)(2,1)S(1)}, u32[]{:S(2)}, u32[]{:S(2)}) collective-permute-start(bf16[256,256]{1,0:T(8,128)(2,1)S(1)} %get-tuple-element.48), channel_id=1, source_target_pairs={{0,1},{1,0},{2,3},{3,2},{4,5},{5,4},{6,7},{7,6},{8,9},{9,8},{10,11... | collective-permute-start | bytes 393224 | tf_op jit(solution)/shard_map/ppermute | solution.py:499
  1.7 14.1 %collective-permute-start.1 = (bf16[256,256]{1,0:T(8,128)(2,1)S(1)}, bf16[256,256]{1,0:T(8,128)(2,1)S(1)}, u32[]{:S(2)}, u32[]{:S(2)}) collective-permute-start(bf16[256,256]{1,0:T(8,128)(2,1)S(1)} %get-tuple-element.49), channel_id=1, source_target_pairs={{0,2},{1,3},{2,0},{3,1},{4,6},{5,7},{6,4},{7,5},{8,10},{9,11},{10,... | collective-permute-start | bytes 393224 | tf_op jit(solution)/shard_map/ppermute | solution.py:499
  4.3 11.5 %collective-permute-start.2 = (bf16[256,256]{1,0:T(8,128)(2,1)S(1)}, bf16[256,256]{1,0:T(8,128)(2,1)S(1)}, u32[]{:S(2)}, u32[]{:S(2)}) collective-permute-start(bf16[256,256]{1,0:T(8,128)(2,1)S(1)} %get-tuple-element.50), channel_id=1, source_target_pairs={{0,3},{1,2},{2,1},{3,0},{4,7},{5,6},{6,5},{7,4},{8,11},{9,10},{10,... | collective-permute-start | bytes 393224 | tf_op jit(solution)/shard_map/ppermute | solution.py:499
  5.3 0.7 copy-start.4
  8.5 2.2 %collective-permute-start.3 = (bf16[48,128]{1,0:T(8,128)(2,1)S(1)}, bf16[48,128]{1,0:T(8,128)(2,1)S(1)}, u32[]{:S(2)}, u32[]{:S(2)}) collective-permute-start(bf16[48,128]{1,0:T(8,128)(2,1)S(1)} %get-tuple-element.52), channel_id=1, source_target_pairs={{0,1},{1,0},{2,3},{3,2},{4,5},{5,4},{6,7},{7,6},{8,9},{9,8},{10,11... | collective-permute-start | bytes 36872 | tf_op jit(solution)/shard_map/ppermute | solution.py:522
  8.7 7.1 %collective-permute-start.4 = (bf16[48,128]{1,0:T(8,128)(2,1)S(1)}, bf16[48,128]{1,0:T(8,128)(2,1)S(1)}, u32[]{:S(2)}, u32[]{:S(2)}) collective-permute-start(bf16[48,128]{1,0:T(8,128)(2,1)S(1)} %get-tuple-element.53), channel_id=1, source_target_pairs={{0,2},{1,3},{2,0},{3,1},{4,6},{5,7},{6,4},{7,5},{8,10},{9,11},{10,... | collective-permute-start | bytes 36872 | tf_op jit(solution)/shard_map/ppermute | solution.py:522
  10.7 5.1 %collective-permute-start.5 = (bf16[48,128]{1,0:T(8,128)(2,1)S(1)}, bf16[48,128]{1,0:T(8,128)(2,1)S(1)}, u32[]{:S(2)}, u32[]{:S(2)}) collective-permute-start(bf16[48,128]{1,0:T(8,128)(2,1)S(1)} %get-tuple-element.54), channel_id=1, source_target_pairs={{0,3},{1,2},{2,1},{3,0},{4,7},{5,6},{6,5},{7,4},{8,11},{9,10},{10,... | collective-permute-start | bytes 36872 | tf_op jit(solution)/shard_map/ppermute | solution.py:522
  20.4 1.6 %collective-permute-start.6 = (bf16[48,3072]{1,0:T(8,128)(2,1)S(1)}, bf16[48,3072]{1,0:T(8,128)(2,1)S(1)}, u32[]{:S(2)}, u32[]{:S(2)}) collective-permute-start(bf16[48,3072]{1,0:T(8,128)(2,1)S(1)} %get-tuple-element.58), channel_id=1, source_target_pairs={{0,1},{1,0},{2,3},{3,2},{4,5},{5,4},{6,7},{7,6},{8,9},{9,8},{10,11... | collective-permute-start | bytes 884744 | tf_op jit(solution)/shard_map/ppermute | solution.py:437
  22.1 6.0 %copy-start = (bf16[24,3072]{1,0:T(8,128)(2,1)S(1)}, bf16[24,3072]{1,0:T(8,128)(2,1)}, u32[]{:S(2)}) copy-start(bf16[24,3072]{1,0:T(8,128)(2,1)} %refs_3_.1) | copy-start | bytes 442372
  22.1 6.0 %copy-start.1 = (bf16[3072,8]{0,1:T(8,128)(2,1)S(1)}, bf16[3072,8]{0,1:T(8,128)(2,1)}, u32[]{:S(2)}) copy-start(bf16[3072,8]{0,1:T(8,128)(2,1)} %param.23) | copy-start | bytes 147460
  22.2 6.0 %copy-start.2 = (f32[3072]{0:T(1024)S(1)}, f32[3072]{0:T(1024)}, u32[]{:S(2)}) copy-start(f32[3072]{0:T(1024)} %param.22) | copy-start | bytes 36868
  22.2 6.0 %copy-start.3 = (s32[24,2]{0,1:T(2,128)S(1)}, s32[24,2]{0,1:T(2,128)}, u32[]{:S(2)}) copy-start(s32[24,2]{0,1:T(2,128)} %param.24) | copy-start | bytes 580
  22.2 6.0 %collective-permute-start.7 = (bf16[24,3072]{1,0:T(8,128)(2,1)S(1)}, bf16[24,3072]{1,0:T(8,128)(2,1)S(1)}, u32[]{:S(2)}, u32[]{:S(2)}) collective-permute-start(bf16[24,3072]{1,0:T(8,128)(2,1)S(1)} %shard_map.140._), channel_id=1, source_target_pairs={{0,2},{1,3},{2,0},{3,1},{4,6},{5,7},{6,4},{7,5},{8,10},{9,11},{10,... | collective-permute-start | bytes 442376 | tf_op jit(solution)/shard_map/ppermute | solution.py:437
  28.7 5.7 %collective-permute-start.8 = (bf16[16,3072]{1,0:T(8,128)(2,1)S(1)}, bf16[16,3072]{1,0:T(8,128)(2,1)S(1)}, u32[]{:S(2)}, u32[]{:S(2)}) collective-permute-start(bf16[16,3072]{1,0:T(8,128)(2,1)S(1)} %get-tuple-element.63), channel_id=1, source_target_pairs={{0,4},{4,0},{8,12},{12,8},{1,5},{5,1},{9,13},{13,9},{2,6},{6,2},{1... | collective-permute-start | bytes 294920 | tf_op jit(solution)/shard_map/ppermute | solution.py:437
  30.4 10.4 %collective-permute-start.9 = (bf16[16,3072]{1,0:T(8,128)(2,1)S(1)}, bf16[16,3072]{1,0:T(8,128)(2,1)S(1)}, u32[]{:S(2)}, u32[]{:S(2)}) collective-permute-start(bf16[16,3072]{1,0:T(8,128)(2,1)S(1)} %get-tuple-element.64), channel_id=1, source_target_pairs={{0,8},{4,12},{8,0},{12,4},{1,9},{5,13},{9,1},{13,5},{2,10},{6,14},... | collective-permute-start | bytes 294920 | tf_op jit(solution)/shard_map/ppermute | solution.py:437
  33.0 8.7 %collective-permute-start.10 = (bf16[16,3072]{1,0:T(8,128)(2,1)S(1)}, bf16[16,3072]{1,0:T(8,128)(2,1)S(1)}, u32[]{:S(2)}, u32[]{:S(2)}) collective-permute-start(bf16[16,3072]{1,0:T(8,128)(2,1)S(1)} %get-tuple-element.65), channel_id=1, source_target_pairs={{0,12},{4,8},{8,4},{12,0},{1,13},{5,9},{9,5},{13,1},{2,14},{6,10},... | collective-permute-start | bytes 294920 | tf_op jit(solution)/shard_map/ppermute | solution.py:437
  33.2 8.5 %collective-permute-start.15 = (bf16[16,3072]{1,0:T(8,128)(2,1)S(1)}, bf16[16,3072]{1,0:T(8,128)(2,1)S(1)}, u32[]{:S(2)}, u32[]{:S(2)}) collective-permute-start(bf16[16,3072]{1,0:T(8,128)(2,1)S(1)} %get-tuple-element.62._.refs_0_), channel_id=1, source_target_pairs={{0,1},{1,0},{2,3},{3,2},{4,5},{5,4},{6,7},{7,6},{8,9},{9,8},{10,11... | collective-permute-start | bytes 294920 | tf_op jit(solution)/shard_map/ppermute | solution.py:437
  33.2 9.7 %collective-permute-start.11 = (bf16[16,3072]{1,0:T(8,128)(2,1)S(1)}, bf16[16,3072]{1,0:T(8,128)(2,1)S(1)}, u32[]{:S(2)}, u32[]{:S(2)}) collective-permute-start(bf16[16,3072]{1,0:T(8,128)(2,1)S(1)} %get-tuple-element.62._.refs_0_), channel_id=1, source_target_pairs={{0,2},{1,3},{2,0},{3,1},{4,6},{5,7},{6,4},{7,5},{8,10},{9,11},{10,... | collective-permute-start | bytes 294920 | tf_op jit(solution)/shard_map/ppermute | solution.py:437
  34.4 9.4 %collective-permute-start.16 = (bf16[16,3072]{1,0:T(8,128)(2,1)S(1)}, bf16[16,3072]{1,0:T(8,128)(2,1)S(1)}, u32[]{:S(2)}, u32[]{:S(2)}) collective-permute-start(bf16[16,3072]{1,0:T(8,128)(2,1)S(1)} %collective-permute-done.8.refs_1_), channel_id=1, source_target_pairs={{0,1},{1,0},{2,3},{3,2},{4,5},{5,4},{6,7},{7,6},{8,9},{9,8},{10,11... | collective-permute-start | bytes 294920 | tf_op jit(solution)/shard_map/ppermute | solution.py:437
  40.8 5.2 %collective-permute-start.12 = (bf16[16,3072]{1,0:T(8,128)(2,1)S(1)}, bf16[16,3072]{1,0:T(8,128)(2,1)S(1)}, u32[]{:S(2)}, u32[]{:S(2)}) collective-permute-start(bf16[16,3072]{1,0:T(8,128)(2,1)S(1)} %collective-permute-done.8.refs_1_), channel_id=1, source_target_pairs={{0,2},{1,3},{2,0},{3,1},{4,6},{5,7},{6,4},{7,5},{8,10},{9,11},{10,... | collective-permute-start | bytes 294920 | tf_op jit(solution)/shard_map/ppermute | solution.py:437
  41.7 4.3 %collective-permute-start.17 = (bf16[16,3072]{1,0:T(8,128)(2,1)S(1)}, bf16[16,3072]{1,0:T(8,128)(2,1)S(1)}, u32[]{:S(2)}, u32[]{:S(2)}) collective-permute-start(bf16[16,3072]{1,0:T(8,128)(2,1)S(1)} %collective-permute-done.9.refs_2_), channel_id=1, source_target_pairs={{0,1},{1,0},{2,3},{3,2},{4,5},{5,4},{6,7},{7,6},{8,9},{9,8},{10,11... | collective-permute-start | bytes 294920 | tf_op jit(solution)/shard_map/ppermute | solution.py:437
  41.7 6.4 %collective-permute-start.13 = (bf16[16,3072]{1,0:T(8,128)(2,1)S(1)}, bf16[16,3072]{1,0:T(8,128)(2,1)S(1)}, u32[]{:S(2)}, u32[]{:S(2)}) collective-permute-start(bf16[16,3072]{1,0:T(8,128)(2,1)S(1)} %collective-permute-done.9.refs_2_), channel_id=1, source_target_pairs={{0,2},{1,3},{2,0},{3,1},{4,6},{5,7},{6,4},{7,5},{8,10},{9,11},{10,... | collective-permute-start | bytes 294920 | tf_op jit(solution)/shard_map/ppermute | solution.py:437
  42.9 6.7 %collective-permute-start.14 = (bf16[16,3072]{1,0:T(8,128)(2,1)S(1)}, bf16[16,3072]{1,0:T(8,128)(2,1)S(1)}, u32[]{:S(2)}, u32[]{:S(2)}) collective-permute-start(bf16[16,3072]{1,0:T(8,128)(2,1)S(1)} %collective-permute-done.10.refs_3_), channel_id=1, source_target_pairs={{0,2},{1,3},{2,0},{3,1},{4,6},{5,7},{6,4},{7,5},{8,10},{9,11},{10,... | collective-permute-start | bytes 294920 | tf_op jit(solution)/shard_map/ppermute | solution.py:437
  43.8 11.0 %collective-permute-start.18 = (bf16[16,3072]{1,0:T(8,128)(2,1)S(1)}, bf16[16,3072]{1,0:T(8,128)(2,1)S(1)}, u32[]{:S(2)}, u32[]{:S(2)}) collective-permute-start(bf16[16,3072]{1,0:T(8,128)(2,1)S(1)} %collective-permute-done.10.refs_3_), channel_id=1, source_target_pairs={{0,1},{1,0},{2,3},{3,2},{4,5},{5,4},{6,7},{7,6},{8,9},{9,8},{10,11... | collective-permute-start | bytes 294920 | tf_op jit(solution)/shard_map/ppermute | solution.py:437
  46.0 8.8 %collective-permute-start.19 = (bf16[16,3072]{1,0:T(8,128)(2,1)S(1)}, bf16[16,3072]{1,0:T(8,128)(2,1)S(1)}, u32[]{:S(2)}, u32[]{:S(2)}) collective-permute-start(bf16[16,3072]{1,0:T(8,128)(2,1)S(1)} %collective-permute-done.11.refs_4_), channel_id=1, source_target_pairs={{0,1},{1,0},{2,3},{3,2},{4,5},{5,4},{6,7},{7,6},{8,9},{9,8},{10,11... | collective-permute-start | bytes 294920 | tf_op jit(solution)/shard_map/ppermute | solution.py:437
  46.0 8.8 %collective-permute-start.20 = (bf16[16,3072]{1,0:T(8,128)(2,1)S(1)}, bf16[16,3072]{1,0:T(8,128)(2,1)S(1)}, u32[]{:S(2)}, u32[]{:S(2)}) collective-permute-start(bf16[16,3072]{1,0:T(8,128)(2,1)S(1)} %collective-permute-done.12.refs_5_), channel_id=1, source_target_pairs={{0,1},{1,0},{2,3},{3,2},{4,5},{5,4},{6,7},{7,6},{8,9},{9,8},{10,11... | collective-permute-start | bytes 294920 | tf_op jit(solution)/shard_map/ppermute | solution.py:437
  48.1 6.8 %collective-permute-start.21 = (bf16[16,3072]{1,0:T(8,128)(2,1)S(1)}, bf16[16,3072]{1,0:T(8,128)(2,1)S(1)}, u32[]{:S(2)}, u32[]{:S(2)}) collective-permute-start(bf16[16,3072]{1,0:T(8,128)(2,1)S(1)} %collective-permute-done.13.refs_6_), channel_id=1, source_target_pairs={{0,1},{1,0},{2,3},{3,2},{4,5},{5,4},{6,7},{7,6},{8,9},{9,8},{10,11... | collective-permute-start | bytes 294920 | tf_op jit(solution)/shard_map/ppermute | solution.py:437
  49.6 5.2 %collective-permute-start.22 = (bf16[16,3072]{1,0:T(8,128)(2,1)S(1)}, bf16[16,3072]{1,0:T(8,128)(2,1)S(1)}, u32[]{:S(2)}, u32[]{:S(2)}) collective-permute-start(bf16[16,3072]{1,0:T(8,128)(2,1)S(1)} %collective-permute-done.14.refs_7_), channel_id=1, source_target_pairs={{0,1},{1,0},{2,3},{3,2},{4,5},{5,4},{6,7},{7,6},{8,9},{9,8},{10,11... | collective-permute-start | bytes 294920 | tf_op jit(solution)/shard_map/ppermute | solution.py:437
  62.0 7.3 %collective-permute-start.23 = (bf16[64,3072]{1,0:T(8,128)(2,1)S(1)}, bf16[64,3072]{1,0:T(8,128)(2,1)S(1)}, u32[]{:S(2)}, u32[]{:S(2)}) collective-permute-start(bf16[64,3072]{1,0:T(8,128)(2,1)S(1)} %get-tuple-element.71), channel_id=1, source_target_pairs={{0,1},{1,0},{2,3},{3,2},{4,5},{5,4},{6,7},{7,6},{8,9},{9,8},{10,11... | collective-permute-start | bytes 1179656 | tf_op jit(solution)/shard_map/ppermute | solution.py:437
  73.5 1.8 %collective-permute-start.28 = (bf16[64,3072]{1,0:T(8,128)(2,1)S(1)}, bf16[64,3072]{1,0:T(8,128)(2,1)S(1)}, u32[]{:S(2)}, u32[]{:S(2)}) collective-permute-start(bf16[64,3072]{1,0:T(8,128)(2,1)S(1)} %get-tuple-element.83), channel_id=1, source_target_pairs={{0,1},{1,0},{2,3},{3,2},{4,5},{5,4},{6,7},{7,6},{8,9},{9,8},{10,11... | collective-permute-start | bytes 1179656 | tf_op jit(solution)/shard_map/ppermute | solution.py:437
  73.6 7.8 %collective-permute-start.24 = (bf16[32,3072]{1,0:T(8,128)(2,1)S(1)}, bf16[32,3072]{1,0:T(8,128)(2,1)S(1)}, u32[]{:S(2)}, u32[]{:S(2)}) collective-permute-start(bf16[32,3072]{1,0:T(8,128)(2,1)S(1)} %shard_map.146.refs_2_), channel_id=1, source_target_pairs={{0,2},{1,3},{2,0},{3,1},{4,6},{5,7},{6,4},{7,5},{8,10},{9,11},{10,... | collective-permute-start | bytes 589832 | tf_op jit(solution)/shard_map/ppermute | solution.py:437
  75.3 10.6 %collective-permute-start.29 = (bf16[32,3072]{1,0:T(8,128)(2,1)S(1)}, bf16[32,3072]{1,0:T(8,128)(2,1)S(1)}, u32[]{:S(2)}, u32[]{:S(2)}) collective-permute-start(bf16[32,3072]{1,0:T(8,128)(2,1)S(1)} %shard_map.150), channel_id=1, source_target_pairs={{0,2},{1,3},{2,0},{3,1},{4,6},{5,7},{6,4},{7,5},{8,10},{9,11},{10,... | collective-permute-start | bytes 589832 | tf_op jit(solution)/shard_map/ppermute | solution.py:437
  81.5 7.6 %collective-permute-start.25 = (bf16[8,3072]{1,0:T(8,128)(2,1)S(1)}, bf16[8,3072]{1,0:T(8,128)(2,1)S(1)}, u32[]{:S(2)}, u32[]{:S(2)}) collective-permute-start(bf16[8,3072]{1,0:T(8,128)(2,1)S(1)} %get-tuple-element.73), channel_id=1, source_target_pairs={{0,4},{4,0},{8,12},{12,8},{1,5},{5,1},{9,13},{13,9},{2,6},{6,2},{1... | collective-permute-start | bytes 147464 | tf_op jit(solution)/shard_map/ppermute | solution.py:655
  81.7 8.8 %collective-permute-start.26 = (bf16[8,3072]{1,0:T(8,128)(2,1)S(1)}, bf16[8,3072]{1,0:T(8,128)(2,1)S(1)}, u32[]{:S(2)}, u32[]{:S(2)}) collective-permute-start(bf16[8,3072]{1,0:T(8,128)(2,1)S(1)} %get-tuple-element.74), channel_id=1, source_target_pairs={{0,8},{4,12},{8,0},{12,4},{1,9},{5,13},{9,1},{13,5},{2,10},{6,14},... | collective-permute-start | bytes 147464 | tf_op jit(solution)/shard_map/ppermute | solution.py:655
  84.6 6.1 %collective-permute-start.27 = (bf16[8,3072]{1,0:T(8,128)(2,1)S(1)}, bf16[8,3072]{1,0:T(8,128)(2,1)S(1)}, u32[]{:S(2)}, u32[]{:S(2)}) collective-permute-start(bf16[8,3072]{1,0:T(8,128)(2,1)S(1)} %get-tuple-element.75), channel_id=1, source_target_pairs={{0,12},{4,8},{8,4},{12,0},{1,13},{5,9},{9,5},{13,1},{2,14},{6,10},... | collective-permute-start | bytes 147464 | tf_op jit(solution)/shard_map/ppermute | solution.py:655
  86.0 4.7 %collective-permute-start.30 = (bf16[8,3072]{1,0:T(8,128)(2,1)S(1)}, bf16[8,3072]{1,0:T(8,128)(2,1)S(1)}, u32[]{:S(2)}, u32[]{:S(2)}) collective-permute-start(bf16[8,3072]{1,0:T(8,128)(2,1)S(1)} %get-tuple-element.86), channel_id=1, source_target_pairs={{0,4},{4,0},{8,12},{12,8},{1,5},{5,1},{9,13},{13,9},{2,6},{6,2},{1... | collective-permute-start | bytes 147464 | tf_op jit(solution)/shard_map/ppermute | solution.py:655
  86.1 5.6 %collective-permute-start.31 = (bf16[8,3072]{1,0:T(8,128)(2,1)S(1)}, bf16[8,3072]{1,0:T(8,128)(2,1)S(1)}, u32[]{:S(2)}, u32[]{:S(2)}) collective-permute-start(bf16[8,3072]{1,0:T(8,128)(2,1)S(1)} %get-tuple-element.87), channel_id=1, source_target_pairs={{0,8},{4,12},{8,0},{12,4},{1,9},{5,13},{9,1},{13,5},{2,10},{6,14},... | collective-permute-start | bytes 147464 | tf_op jit(solution)/shard_map/ppermute | solution.py:655
  89.1 5.9 %collective-permute-start.32 = (bf16[8,3072]{1,0:T(8,128)(2,1)S(1)}, bf16[8,3072]{1,0:T(8,128)(2,1)S(1)}, u32[]{:S(2)}, u32[]{:S(2)}) collective-permute-start(bf16[8,3072]{1,0:T(8,128)(2,1)S(1)} %get-tuple-element.88), channel_id=1, source_target_pairs={{0,12},{4,8},{8,4},{12,0},{1,13},{5,9},{9,5},{13,1},{2,14},{6,10},... | collective-permute-start | bytes 147464 | tf_op jit(solution)/shard_map/ppermute | solution.py:655
where the time goes:
time: 96.4 us; the launch traced here: 95.9 us
  Pallas kernels  41.4 us (43%)
  starting transfers between devices  28.3 us (29%)
  waiting for transfers between devices  23.6 us (24%)
  local copies, waits for them, and re-layouts  1.63 us (2%)
    pallas_call x16, Pallas kernels, call(): pl.pallas_call(kernel, in_specs=specs, out_specs=[VMEM] * len(outs), out_...  40.5 us
    ppermute x21, waiting for transfers between devices, send_to(): return lax.ppermute(x, axis, xor_pairs(lax.axis_size(axis), distance))  19 us
    ppermute x21, starting transfers between devices, send_to(): return lax.ppermute(x, axis, xor_pairs(lax.axis_size(axis), distance))  13.3 us
    ppermute x6, starting transfers between devices, on_device(): lax.ppermute(pieces[d], 'exp', xor_pairs(groups, d))  8.9 us
    ppermute x6, waiting for transfers between devices, on_device(): lax.ppermute(pieces[d], 'exp', xor_pairs(groups, d))  4.54 us
    ppermute x3, starting transfers between devices, on_device(): lax.ppermute(packed[d], 'ten', xor_pairs(ten, d))  3.18 us
    ppermute x3, starting transfers between devices, on_device(): lax.ppermute(decoded[d], 'ten', xor_pairs(ten, d))  2.95 us
  transfers between devices with their start and end apart: 33, of which 11 were waited for; matrix products, arithmetic and copies ran while one was open for 1% of the time, Pallas kernels for 24%

commit v1 on v0

--- a/solution.py
+++ b/solution.py
@@ -94,21 +94,32 @@
             base += prefix_rows
 
 
-def decode_kernel(len_ref, q_ref, kv_hbm, new_hbm, *refs, per_kv, span_dev):
-    out_refs, (kv_ref, new_ref, scratch, sems) = refs[:-4], refs[-4:]
-    for copy in load_all(((kv_hbm, kv_ref), (new_hbm, new_ref)), sems):
+def decode_kernel(len_hbm, q_hbm, kv_hbm, new_hbm, w_hbm, *refs, per_kv, span_dev, block):
+    out_refs, (w_low, len_ref, q_ref, kv_ref, new_ref, q_heads, scratch, sems) = refs[:-8], refs[-8:]
+    q_rows = q_hbm.at[pl.ds(q_hbm.shape[0] - block, block)]
+    pairs = ((len_hbm, len_ref), (q_rows, q_ref), (kv_hbm, kv_ref), (new_hbm, new_ref))
+    loads = load_all(pairs, sems)
+    w_copy = pltpu.make_async_copy(
+        w_hbm.at[:, pl.ds(0, w_low.shape[1])], w_low, sems.at[len(pairs)]
+    )
+    w_copy.start()
+    for copy in loads:
         copy.wait()
     me = lax.axis_index("ten")
     dec_dev, ctx_len, kv_width = kv_ref.shape[1:]
-    heads = q_ref.shape[0] // dec_dev
+    heads = q_ref.shape[1] // HD
     heads_kv = kv_width // HD
+    for h in range(heads):
+        q_heads[h * dec_dev : (h + 1) * dec_dev, :] = q_ref[
+            block - dec_dev :, h * HD : (h + 1) * HD
+        ].astype(F32)
     scale = HD ** (-0.5)
     row_group = lax.broadcasted_iota(jnp.int32, (heads, kv_width), 0) // per_kv
     lane_group = lax.broadcasted_iota(jnp.int32, (heads, kv_width), 1) // HD
     own = row_group == lane_group
     position = lax.broadcasted_iota(jnp.int32, (heads, ctx_len), 1)
     for r in range(dec_dev):
-        q = q_ref[r * heads : (r + 1) * heads, :]
+        q = q_heads[pl.ds(r, heads, stride=dec_dev), :].astype(BF16)
         wide = jnp.where(own, jnp.concatenate([q] * heads_kv, axis=1), jnp.zeros((), BF16))
         scores = (
             lax.dot_general(
@@ -135,12 +146,13 @@
     chunk = scratch.shape[0] // len(out_refs)
     for d, out in enumerate(out_refs):
         out[...] = scratch[pl.ds(pl.multiple_of((me ^ d) * chunk, 4), chunk), :].astype(BF16)
+    w_copy.wait()
 
 
 def attend_kernel(len_ref, *refs, ten, rows, prefix_rows, span_dev, heads_own, kv_own):
     packed, decoded = refs[:ten], refs[ten : 2 * ten]
-    w_ref, ahead_ref, _ = refs[2 * ten : 2 * ten + 3]
-    keep_ref, send_ref, ahead_out, att, sem = refs[2 * ten + 3 :]
+    w_ref, ahead_ref = refs[2 * ten : 2 * ten + 2]
+    keep_ref, send_ref, ahead_out, att, sem = refs[2 * ten + 2 :]
     copy = pltpu.make_async_copy(ahead_ref.at[0], ahead_out, sem)
     copy.start()
     me = lax.axis_index("ten")
@@ -279,12 +291,11 @@
 
 
 def hidden_kernel(*refs, pieces, expert, tile, resident, last):
-    xs, refs = refs[:pieces], refs[pieces:]
+    xs, gate_refs, refs = refs[:pieces], refs[pieces : pieces + 2], refs[pieces + 2 :]
     if resident:
-        gate_ref, up_ref, refs = refs[0], refs[1], refs[2:]
+        up_ref, refs = refs[0], refs[1:]
     else:
-        gate_low, gate_high, up_low, up_hbm, down_hbm = refs[:5]
-        refs = refs[5:]
+        up_low, up_hbm, down_hbm, refs = refs[0], refs[1], refs[2], refs[3:]
     if not last:
         next_gate, refs = refs[0], refs[1:]
     hidden_ref, refs = refs[0], refs[1:]
@@ -292,48 +303,55 @@
         up_rest, down_low, refs = refs[0], refs[1], refs[2:]
     if not last:
         next_low, refs = refs[0], refs[1:]
-    x_all, sems = refs
-    pending = []
-
-    def start(source, target, n):
-        pending.append(pltpu.make_async_copy(source, target, sems.at[n]))
-        pending[-1].start()
-
+    x_all, gates, sems = refs
     tiles = hidden_ref.shape[1] // tile
-    up_copies = []
+    stream, position = [], [0]
     if not resident:
-        for i in range(1, tiles):
-            up_copies.append(
-                pltpu.make_async_copy(
-                    up_hbm.at[expert, :, pl.ds(i * tile, tile)],
-                    up_rest.at[:, pl.ds((i - 1) * tile, tile)],
-                    sems.at[i],
+        for i in range(tiles - 1):
+            stream.append(
+                (
+                    up_hbm.at[expert, :, pl.ds((i + 1) * tile, tile)],
+                    up_rest.at[:, pl.ds(i * tile, tile)],
                 )
             )
-            up_copies[-1].start()
+        for i in range(down_low.shape[1] // tile):
+            cols = pl.ds(i * tile, tile)
+            stream.append((down_hbm.at[expert, :, cols], down_low.at[:, cols]))
     if not last:
-        start(next_gate.at[expert + 1, :, pl.ds(0, next_low.shape[1])], next_low, 0)
+        stream.append((next_gate.at[expert + 1, :, pl.ds(0, next_low.shape[1])], next_low))
+    copies = [pltpu.make_async_copy(a, b, sems.at[i]) for i, (a, b) in enumerate(stream)]
+
+    def advance(count):
+        for copy in copies[position[0] : position[0] + count]:
+            copy.start()
+        position[0] = min(position[0] + count, len(copies))
+
+    advance(3)
     for i, p in enumerate(xs):
         x_all[i * SLOTS : (i + 1) * SLOTS, :] = p[expert * SLOTS : (expert + 1) * SLOTS, :]
+    first_width = gate_refs[0].shape[1]
+    for i in range(tiles):
+        start = i * tile
+        if start < first_width:
+            gate_tile = gate_refs[0][:, start : start + tile]
+        else:
+            gate_tile = gate_refs[1][:, start - first_width : start - first_width + tile]
+        gate = jnp.dot(x_all[...], gate_tile, preferred_element_type=F32)
+        gates[:, start : start + tile] = gate / (1.0 + jnp.exp(-gate))
     for i in range(tiles):
         cols = slice(i * tile, (i + 1) * tile)
-        if resident:
-            gate_tile = gate_ref[:, cols]
-        else:
-            gate_tile = gate_low[:, cols] if i < tiles - 1 else gate_high[...]
-        gate = jnp.dot(x_all[...], gate_tile, preferred_element_type=F32)
         if resident:
             up_tile = up_ref[:, cols]
         elif i == 0:
             up_tile = up_low[...]
         else:
-            up_copies[i - 1].wait()
-            if i == tiles - 1:
-                start(down_hbm.at[expert, :, pl.ds(0, down_low.shape[1])], down_low, tiles)
+            copies[i - 1].wait()
+            advance(1)
             up_tile = up_rest[:, (i - 1) * tile : i * tile]
         up = jnp.dot(x_all[...], up_tile, preferred_element_type=F32)
-        hidden_ref[:, cols] = (gate / (1.0 + jnp.exp(-gate)) * up).astype(BF16)
-    for copy in pending:
+        hidden_ref[:, cols] = (gates[:, cols] * up).astype(BF16)
+    advance(len(copies))
+    for copy in copies[0 if resident else tiles - 1 :]:
         copy.wait()
 
 
@@ -370,12 +388,15 @@
                     sems.at[2 + i],
                 )
             )
-            copies[-1].start()
+        for copy in copies[:3]:
+            copy.start()
     for start in range(0, width, tile):
         cols = slice(start, start + tile)
         if start >= split:
             i = (start - split) // tile
             copies[i].wait()
+            for copy in copies[i + 3 : i + 4]:
+                copy.start()
             down_tile = rest_ref[:, i * tile : (i + 1) * tile]
         else:
             down_tile = down_ref[:, cols]
@@ -386,10 +407,10 @@
         copy.wait()
 
 
-def add_kernel(*refs, parts, first, rows, skip=0):
+def add_kernel(*refs, parts, firsts, rows, skip=0):
     addends, outs = refs[:parts], refs[parts + skip :]
-    total = addends[0][first : first + rows, :].astype(F32)
-    for a in addends[1:]:
+    total = addends[0][firsts[0] : firsts[0] + rows, :].astype(F32)
+    for a, first in zip(addends[1:], firsts[1:]):
         total = total + a[first : first + rows, :].astype(F32)
     each = outs[0].shape[0]
     for i, out in enumerate(outs):
@@ -413,18 +434,18 @@
     out[...] = (residual_ref[...] + total).astype(out.dtype)
 
 
-def fetch_kernel(source_ref, _, out_ref, token_ref, sem, *, expert):
+def fetch_kernel(source_ref, _, out_ref, token_ref, sem, *, expert, first):
     source = source_ref if expert is None else source_ref.at[expert]
-    copy = pltpu.make_async_copy(source.at[:, pl.ds(0, out_ref.shape[1])], out_ref, sem)
+    copy = pltpu.make_async_copy(source.at[:, pl.ds(first, out_ref.shape[1])], out_ref, sem)
     copy.start()
     token_ref[...] = jnp.zeros_like(token_ref)
     copy.wait()
 
 
-def fetch(source, expert, after, columns=None):
+def fetch(source, expert, after, columns=None, first=0):
     rows, width = source.shape[-2:]
     return call(
-        functools.partial(fetch_kernel, expert=expert),
+        functools.partial(fetch_kernel, expert=expert, first=first),
         (source, after),
         [HBM, VMEM],
         [out((rows, columns or width), BF16), out((8, HD), F32)],
@@ -437,23 +458,29 @@
     return lax.ppermute(x, axis, xor_pairs(lax.axis_size(axis), distance))
 
 
-def halves_down(keep, send, axis, size):
+def halves_down(keep, send, axis, size, cuts=1):
     addends = [keep]
     rows = keep.shape[0]
-    last_sent = send
-    for bit in up_bits(size):
+    for bit in up_bits(size)[:-1]:
         addends.append(send_to(send, axis, bit))
-        last_sent = send
-        if bit * 2 < size:
-            rows //= 2
-            send = call(
-                functools.partial(add_kernel, parts=len(addends), first=rows, rows=rows),
-                addends,
-                [VMEM] * len(addends),
-                [out((rows, keep.shape[1]), BF16)],
-                limit=3,
-            )[0]
-    return addends, rows, last_sent
+        rows //= 2
+        parts = cuts if bit * 4 == size else 1
+        sends = call(
+            functools.partial(
+                add_kernel, firsts=[rows] * len(addends), rows=rows, parts=len(addends)
+            ),
+            addends,
+            [VMEM] * len(addends),
+            [out((rows // parts, keep.shape[1]), BF16)] * parts,
+            limit=3,
+        )
+        send = sends[0]
+    share = rows // cuts
+    result = []
+    for c in reversed(range(cuts)):
+        got = send_to(sends[c], axis, size // 2)
+        result.append([(a, c * share) for a in addends] + [(got, 0)])
+    return result[::-1], share, sends[-1]
 
 
 def on_device(
@@ -499,30 +526,26 @@
         lax.ppermute(packed[d], "ten", xor_pairs(ten, d)) for d in range(1, ten)
     ]
 
-    decoded = call(
-        functools.partial(decode_kernel, per_kv=per_kv, span_dev=span_dev),
-        (
-            decode_len,
-            queries[span_dev:].reshape(dec_dev * heads_q, HD),
-            decode_kv,
-            new_kv,
-        ),
-        [SMEM, VMEM, HBM, HBM],
-        [out((heads_own * dec_dev, HD), BF16)] * ten,
+    q_block = -(-dec_dev // 8) * 8
+    *decoded, proj = call(
+        functools.partial(decode_kernel, per_kv=per_kv, span_dev=span_dev, block=q_block),
+        (decode_len, queries, decode_kv, new_kv, out_proj),
+        [HBM] * 5,
+        [out((heads_own * dec_dev, HD), BF16)] * ten + [out(out_proj.shape, BF16)],
         [
+            pltpu.SMEM(decode_len.shape, jnp.int32),
+            pltpu.VMEM((q_block, queries.shape[1]), BF16),
             pltpu.VMEM(decode_kv.shape, BF16),
             pltpu.VMEM(new_kv.shape, BF16),
             pltpu.VMEM((heads_q * dec_dev, HD), F32),
-            pltpu.SemaphoreType.DMA((2,)),
+            pltpu.VMEM((heads_q * dec_dev, HD), F32),
+            pltpu.SemaphoreType.DMA((5,)),
         ],
-        limit=4,
-    )
-    own_decoded = decoded[0]
+        limit=5,
+    )
     decoded = [decoded[0]] + [
         lax.ppermute(decoded[d], "ten", xor_pairs(ten, d)) for d in range(1, ten)
     ]
-    proj, proj_token = fetch(out_proj, None, own_decoded)
-
     half = ten * rows // 2
     keep, send, up = call(
         functools.partial(
@@ -534,8 +557,8 @@
             heads_own=heads_own,
             kv_own=kv_own,
         ),
-        (prefix_len, *packed, *decoded, held(proj), w_up, proj_token),
-        [SMEM] + [VMEM] * (2 * ten) + [VMEM, HBM, VMEM],
+        (prefix_len, *packed, *decoded, held(proj), w_up),
+        [SMEM] + [VMEM] * (2 * ten) + [VMEM, HBM],
         [
             out((half, width), F32),
             out((half, width), BF16),
@@ -544,7 +567,8 @@
         [pltpu.VMEM((ten * rows, heads_own * HD), F32), pltpu.SemaphoreType.DMA],
         limit=4,
     )
-    addends, _, last_sent = halves_down(keep, send, "ten", ten)
+    (addends,), _, last_sent = halves_down(keep, send, "ten", ten)
+    addends = [a for a, _ in addends]
     down, down_token = fetch(w_down, 0, last_sent)
 
     routed = call(
@@ -570,8 +594,10 @@
     for bit in reversed(up_bits(ten)):
         block = block + [send_to(b, "ten", bit) for b in block]
 
-    gate, _ = fetch(w_gate, 0, slots[0])
     hidden_units = w_gate.shape[2]
+    gate_half = hidden_units // 2
+    gate_a, gate_token = fetch(w_gate, 0, slots[0], gate_half)
+    gate_b, _ = fetch(w_gate, 0, gate_token, gate_half, gate_half)
     tile = min(512, hidden_units // 4)
     tiles = hidden_units // tile
     down_low_width = 2 * tile
@@ -582,8 +608,8 @@
         args, specs = [*block], [VMEM] * len(block)
         outs = [out((2 * half, hidden_units), BF16)]
         if resident:
-            args += [held(gate), held(up)]
-            specs += [VMEM] * 2
+            args += [held(gate_a), held(gate_b), held(up)]
+            specs += [VMEM] * 3
         else:
             args += [held(next_low), held(gate_high), held(up_low), w_up, w_down]
             specs += [VMEM] * 3 + [HBM] * 2
@@ -607,7 +633,11 @@
             args,
             specs,
             outs,
-            [pltpu.VMEM((2 * half, width), BF16), pltpu.SemaphoreType.DMA((tiles + 1,))],
+            [
+                pltpu.VMEM((2 * half, width), BF16),
+                pltpu.VMEM((2 * half, hidden_units), F32),
+                pltpu.SemaphoreType.DMA((tiles + 4,)),
+            ],
             limit=3,
             flops=8 * half * width * hidden_units,
         )
@@ -640,20 +670,30 @@
         if not last:
             gate_high, up_low = rest[-2:]
             rest = rest[:-2]
-        addends, share, before = halves_down(keep, send, "ten", ten)
-        pieces = call(
-            functools.partial(
-                add_kernel, parts=len(addends), first=0, rows=share, skip=len(rest)
-            ),
-            (*addends, *rest),
-            [VMEM] * (len(addends) + len(rest)),
-            [out((SLOTS, width), BF16)] * groups,
-            limit=3,
-        )
-        returned.append(pieces[0])
-        returned += [
-            lax.ppermute(pieces[d], "exp", xor_pairs(groups, d)) for d in range(1, groups)
-        ]
+        cuts = 2 if groups > 2 else 1
+        shares, share, before = halves_down(keep, send, "ten", ten, cuts)
+        mine = [None] * groups
+        each = groups // cuts
+        for c in reversed(range(cuts)):
+            addends = [a for a, _ in shares[c]]
+            unused = rest if c == 0 else []
+            pieces = call(
+                functools.partial(
+                    add_kernel,
+                    parts=len(addends),
+                    firsts=[first for _, first in shares[c]],
+                    rows=share,
+                    skip=len(unused),
+                ),
+                (*addends, *unused),
+                [VMEM] * (len(addends) + len(unused)),
+                [out((SLOTS, width), BF16)] * each,
+                limit=3,
+            )
+            for i in reversed(range(each)):
+                d = c * each + i
+                mine[d] = send_to(pieces[i], "exp", d) if d else pieces[i]
+        returned += mine
     return pl.pallas_call(
         functools.partial(mix_kernel, local=local, groups=groups),
         in_specs=[VMEM] * (2 + len(returned)),

time: 96.4 us -> 92.7 us (0.962)
  local copies, waits for them, and re-layouts: 1.63 us -> 0.03 us
  Pallas kernels: 41.4 us -> 39.9 us
    ppermute x21 -> x29, starting transfers between devices: 13.3 us -> 22.2 us  [send_to(): return lax.ppermute(x, axis, xor_pairs(lax.axis_size(axis), distance))]
    ppermute x6 -> x0, starting transfers between devices: 8.9 us -> none  [on_device(): lax.ppermute(pieces[d], 'exp', xor_pairs(groups, d))]
    ppermute x6 -> x0, waiting for transfers between devices: 4.54 us -> none  [on_device(): lax.ppermute(pieces[d], 'exp', xor_pairs(groups, d))]
    ppermute x21 -> x29, waiting for transfers between devices: 19 us -> 21.4 us  [send_to(): return lax.ppermute(x, axis, xor_pairs(lax.axis_size(axis), distance))]
    ppermute x3, waiting for transfers between devices: 0.01 us -> 1.77 us  [on_device(): lax.ppermute(decoded[d], 'ten', xor_pairs(ten, d))]
    pallas_call x16 -> x18, Pallas kernels: 40.5 us -> 39 us  [call(): pl.pallas_call(kernel, in_specs=specs, out_specs=[VMEM] * len(outs), out_...]
  transfers between devices with their start and end apart: 33 -> 35, of which waited for: 11 -> 14; matrix products, arithmetic and copies ran while one was open for 1% -> 0% of each run, Pallas kernels for 24% -> 22%
where the time goes in v1:
time: 92.7 us; the launch traced here: 92.4 us
  Pallas kernels  39.9 us (43%)
  starting transfers between devices  28.4 us (31%)
  waiting for transfers between devices  23.2 us (25%)
    pallas_call x18, Pallas kernels, call(): pl.pallas_call(kernel, in_specs=specs, out_specs=[VMEM] * len(outs), out_...  39 us
    ppermute x29, starting transfers between devices, send_to(): return lax.ppermute(x, axis, xor_pairs(lax.axis_size(axis), distance))  22.2 us
    ppermute x29, waiting for transfers between devices, send_to(): return lax.ppermute(x, axis, xor_pairs(lax.axis_size(axis), distance))  21.4 us
    ppermute x3, starting transfers between devices, on_device(): lax.ppermute(packed[d], 'ten', xor_pairs(ten, d))  3.18 us
    ppermute x3, starting transfers between devices, on_device(): lax.ppermute(decoded[d], 'ten', xor_pairs(ten, d))  2.95 us
  transfers between devices with their start and end apart: 35, of which 14 were waited for; matrix products, arithmetic and copies ran while one was open for 0% of the time, Pallas kernels for 22%

profile of v1, /device:TPU:0, one launch (start us, length us, event | category | flops | bytes accessed | tf_op | source)
XLA Modules:
  0.0 92.4 jit_solution(6816863510537287098)
XLA Ops:
  0.0 1.1 %shard_map.136 = (bf16[256,256]{1,0:T(8,128)(2,1)S(1)}, bf16[256,256]{1,0:T(8,128)(2,1)S(1)}, bf16[256,256]{1,0:T(8,128)(2,1)S(1)}, bf16[256,256]{1,0:T(8,128)(2,1)S(1)}) custom-call(bf16[24,6144]{1,0:T(8,128)(2,1)} %q_hbm.3, bf16[2,24,1024]{2,1,0:T(8,128)(2,1)} %new_hbm.3, bf16[2,1,32,1024]{3,2,1,0:T(8,128)(2,1)} %prefix_hbm.1), custom_call_target="tpu_custom_call" | custom-call | tf_op jit(solution)/shard_map/pallas_call | solution.py:51
  1.1 0.6 collective-permute-start
  1.7 2.6 %collective-permute-start.1 = (bf16[256,256]{1,0:T(8,128)(2,1)S(1)}, bf16[256,256]{1,0:T(8,128)(2,1)S(1)}, u32[]{:S(2)}, u32[]{:S(2)}) collective-permute-start(bf16[256,256]{1,0:T(8,128)(2,1)S(1)} %get-tuple-element.54), channel_id=1, source_target_pairs={{0,2},{1,3},{2,0},{3,1},{4,6},{5,7},{6,4},{7,5},{8,10},{9,11},{10,... | collective-permute-start | bytes 393224 | tf_op jit(solution)/shard_map/ppermute | solution.py:526
  4.3 0.0 collective-permute-start.2
  4.3 4.1 %shard_map.137 = (bf16[48,128]{1,0:T(8,128)(2,1)S(1)}, bf16[48,128]{1,0:T(8,128)(2,1)S(1)}, bf16[48,128]{1,0:T(8,128)(2,1)S(1)}, bf16[48,128]{1,0:T(8,128)(2,1)S(1)}, bf16[1536,3072]{1,0:T(8,128)(2,1)S(1)}) custom-call(s32[4]{0:T(128)} %len_hbm.1, bf16[24,6144]{1,0:T(8,128)(2,1)} %q_hbm.3, bf16[2,4,48,1024]{3,2,1,0:T(8,128)(2,1)} %kv_hbm.1, ...), custom_call_target="tpu_custom_call" | custom-call | tf_op jit(solution)/shard_map/pallas_call | solution.py:51
  8.4 0.2 collective-permute-start.3
  8.6 1.9 %collective-permute-start.4 = (bf16[48,128]{1,0:T(8,128)(2,1)S(1)}, bf16[48,128]{1,0:T(8,128)(2,1)S(1)}, u32[]{:S(2)}, u32[]{:S(2)}) collective-permute-start(bf16[48,128]{1,0:T(8,128)(2,1)S(1)} %get-tuple-element.58), channel_id=1, source_target_pairs={{0,2},{1,3},{2,0},{3,1},{4,6},{5,7},{6,4},{7,5},{8,10},{9,11},{10,... | collective-permute-start | bytes 36872 | tf_op jit(solution)/shard_map/ppermute | solution.py:547
  10.6 0.8 collective-permute-start.5
  12.0 0.3 collective-permute-done.4.refs_6_
  12.3 1.5 %collective-permute-done.5.refs_7_ = bf16[48,128]{1,0:T(8,128)(2,1)S(1)} collective-permute-done((bf16[48,128]{1,0:T(8,128)(2,1)S(1)}, bf16[48,128]{1,0:T(8,128)(2,1)S(1)}, u32[]{:S(2)}, u32[]{:S(2)}) %collective-permute-start.5) | collective-permute-done | bytes 12320 | tf_op jit(solution)/shard_map/ppermute | solution.py:547
  13.8 0.0 collective-permute-done.refs_1_
  13.8 0.0 collective-permute-done.1.refs_2_
  13.8 0.0 collective-permute-done.2.refs_3_
  13.8 4.6 %shard_map.138 = (f32[48,3072]{1,0:T(8,128)S(1)}, bf16[48,3072]{1,0:T(8,128)(2,1)S(1)}, bf16[3072,2048]{1,0:T(8,128)(2,1)S(1)}) custom-call(s32[1]{0:T(128)S(6)} %copy.15.len_ref, bf16[256,256]{1,0:T(8,128)(2,1)S(1)} %get-tuple-element.52.refs_0_, bf16[256,256]{1,0:T(8,128)(2,1)S(1)} %collective-permute-done.refs_1_, ...), custom_call_target="tpu_custom_call" | custom-call | tf_op jit(solution)/shard_map/pallas_call | solution.py:51
  18.4 0.2 collective-permute-start.6
  18.6 1.5 %collective-permute-done.6.refs_1_ = bf16[48,3072]{1,0:T(8,128)(2,1)S(1)} collective-permute-done((bf16[48,3072]{1,0:T(8,128)(2,1)S(1)}, bf16[48,3072]{1,0:T(8,128)(2,1)S(1)}, u32[]{:S(2)}, u32[]{:S(2)}) %collective-permute-start.6) | collective-permute-done | bytes 294944 | tf_op jit(solution)/shard_map/ppermute | solution.py:458
  20.1 0.0 copy-start
  20.1 0.0 copy-start.1
  20.1 0.0 copy-start.2
  20.1 0.0 copy-start.3
  20.1 0.8 collective-permute-start.7
  20.9 4.6 %shard_map.140 = (bf16[2048,3072]{1,0:T(8,128)(2,1)S(1)}, f32[8,128]{1,0:T(8,128)S(1)}) custom-call(bf16[2,2048,3072]{2,1,0:T(8,128)(2,1)} %refs_0_.3, bf16[24,3072]{1,0:T(8,128)(2,1)S(1)} %shard_map.139._), custom_call_target="tpu_custom_call" | custom-call | tf_op jit(solution)/shard_map/pallas_call | solution.py:51
  25.5 0.5 collective-permute-done.7.refs_2_
  26.1 0.6 shard_map.141
  26.6 1.6 %collective-permute-start.8 = (bf16[16,3072]{1,0:T(8,128)(2,1)S(1)}, bf16[16,3072]{1,0:T(8,128)(2,1)S(1)}, u32[]{:S(2)}, u32[]{:S(2)}) collective-permute-start(bf16[16,3072]{1,0:T(8,128)(2,1)S(1)} %get-tuple-element.67), channel_id=1, source_target_pairs={{0,4},{4,0},{8,12},{12,8},{1,5},{5,1},{9,13},{13,9},{2,6},{6,2},{1... | collective-permute-start | bytes 294920 | tf_op jit(solution)/shard_map/ppermute | solution.py:458
  28.3 2.6 %collective-permute-start.9 = (bf16[16,3072]{1,0:T(8,128)(2,1)S(1)}, bf16[16,3072]{1,0:T(8,128)(2,1)S(1)}, u32[]{:S(2)}, u32[]{:S(2)}) collective-permute-start(bf16[16,3072]{1,0:T(8,128)(2,1)S(1)} %get-tuple-element.68), channel_id=1, source_target_pairs={{0,8},{4,12},{8,0},{12,4},{1,9},{5,13},{9,1},{13,5},{2,10},{6,14},... | collective-permute-start | bytes 294920 | tf_op jit(solution)/shard_map/ppermute | solution.py:458
  30.9 0.2 collective-permute-start.10
  31.1 1.0 %collective-permute-start.11 = (bf16[16,3072]{1,0:T(8,128)(2,1)S(1)}, bf16[16,3072]{1,0:T(8,128)(2,1)S(1)}, u32[]{:S(2)}, u32[]{:S(2)}) collective-permute-start(bf16[16,3072]{1,0:T(8,128)(2,1)S(1)} %get-tuple-element.66._.refs_0_), channel_id=1, source_target_pairs={{0,2},{1,3},{2,0},{3,1},{4,6},{5,7},{6,4},{7,5},{8,10},{9,11},{10,... | collective-permute-start | bytes 294920 | tf_op jit(solution)/shard_map/ppermute | solution.py:458
  32.1 0.2 collective-permute-done.8.refs_1_
  32.3 0.0 collective-permute-start.16
  32.3 6.1 %collective-permute-done.9.refs_2_ = bf16[16,3072]{1,0:T(8,128)(2,1)S(1)} collective-permute-done((bf16[16,3072]{1,0:T(8,128)(2,1)S(1)}, bf16[16,3072]{1,0:T(8,128)(2,1)S(1)}, u32[]{:S(2)}, u32[]{:S(2)}) %collective-permute-start.9) | collective-permute-done | bytes 98336 | tf_op jit(solution)/shard_map/ppermute | solution.py:458
  38.4 1.1 %collective-permute-start.12 = (bf16[16,3072]{1,0:T(8,128)(2,1)S(1)}, bf16[16,3072]{1,0:T(8,128)(2,1)S(1)}, u32[]{:S(2)}, u32[]{:S(2)}) collective-permute-start(bf16[16,3072]{1,0:T(8,128)(2,1)S(1)} %collective-permute-done.8.refs_1_), channel_id=1, source_target_pairs={{0,2},{1,3},{2,0},{3,1},{4,6},{5,7},{6,4},{7,5},{8,10},{9,11},{10,... | collective-permute-start | bytes 294920 | tf_op jit(solution)/shard_map/ppermute | solution.py:458
  39.5 1.0 %collective-permute-start.13 = (bf16[16,3072]{1,0:T(8,128)(2,1)S(1)}, bf16[16,3072]{1,0:T(8,128)(2,1)S(1)}, u32[]{:S(2)}, u32[]{:S(2)}) collective-permute-start(bf16[16,3072]{1,0:T(8,128)(2,1)S(1)} %collective-permute-done.9.refs_2_), channel_id=1, source_target_pairs={{0,2},{1,3},{2,0},{3,1},{4,6},{5,7},{6,4},{7,5},{8,10},{9,11},{10,... | collective-permute-start | bytes 294920 | tf_op jit(solution)/shard_map/ppermute | solution.py:458
  40.5 0.0 collective-permute-done.11.refs_4_
  40.5 1.1 %collective-permute-start.14 = (bf16[16,3072]{1,0:T(8,128)(2,1)S(1)}, bf16[16,3072]{1,0:T(8,128)(2,1)S(1)}, u32[]{:S(2)}, u32[]{:S(2)}) collective-permute-start(bf16[16,3072]{1,0:T(8,128)(2,1)S(1)} %collective-permute-done.10.refs_3_), channel_id=1, source_target_pairs={{0,2},{1,3},{2,0},{3,1},{4,6},{5,7},{6,4},{7,5},{8,10},{9,11},{10,... | collective-permute-start | bytes 294920 | tf_op jit(solution)/shard_map/ppermute | solution.py:458
  41.6 0.0 collective-permute-start.18
  41.6 1.9 %collective-permute-done.12.refs_5_ = bf16[16,3072]{1,0:T(8,128)(2,1)S(1)} collective-permute-done((bf16[16,3072]{1,0:T(8,128)(2,1)S(1)}, bf16[16,3072]{1,0:T(8,128)(2,1)S(1)}, u32[]{:S(2)}, u32[]{:S(2)}) %collective-permute-start.12) | collective-permute-done | bytes 98336 | tf_op jit(solution)/shard_map/ppermute | solution.py:458
  43.5 0.5 collective-permute-start.20
  44.0 1.6 %collective-permute-done.13.refs_6_ = bf16[16,3072]{1,0:T(8,128)(2,1)S(1)} collective-permute-done((bf16[16,3072]{1,0:T(8,128)(2,1)S(1)}, bf16[16,3072]{1,0:T(8,128)(2,1)S(1)}, u32[]{:S(2)}, u32[]{:S(2)}) %collective-permute-start.13) | collective-permute-done | bytes 98336 | tf_op jit(solution)/shard_map/ppermute | solution.py:458
  45.6 1.7 %collective-permute-done.14.refs_7_ = bf16[16,3072]{1,0:T(8,128)(2,1)S(1)} collective-permute-done((bf16[16,3072]{1,0:T(8,128)(2,1)S(1)}, bf16[16,3072]{1,0:T(8,128)(2,1)S(1)}, u32[]{:S(2)}, u32[]{:S(2)}) %collective-permute-start.14) | collective-permute-done | bytes 98336 | tf_op jit(solution)/shard_map/ppermute | solution.py:458
  47.3 2.8 %shard_map.142 = (bf16[3072,1024]{1,0:T(8,128)(2,1)S(1)}, f32[8,128]{1,0:T(8,128)S(1)}) custom-call(bf16[2,3072,2048]{2,1,0:T(8,128)(2,1)} %refs_0_.2, bf16[16,3072]{1,0:T(8,128)(2,1)S(1)} %get-tuple-element.66._.refs_0_), custom_call_target="tpu_custom_call" | custom-call | tf_op jit(solution)/shard_map/pallas_call | solution.py:51
  50.1 3.4 %shard_map.143 = (bf16[3072,1024]{1,0:T(8,128)(2,1)S(1)}, f32[8,128]{1,0:T(8,128)}) custom-call(bf16[2,3072,2048]{2,1,0:T(8,128)(2,1)} %refs_0_.2, f32[8,128]{1,0:T(8,128)S(1)} %get-tuple-element.71._), custom_call_target="tpu_custom_call" | custom-call | tf_op jit(solution)/shard_map/pallas_call | solution.py:51
  53.5 4.6 %shard_map.144 = (bf16[128,2048]{1,0:T(8,128)(2,1)S(1)}, bf16[3072,1536]{1,0:T(8,128)(2,1)S(1)}) custom-call(bf16[16,3072]{1,0:T(8,128)(2,1)S(1)} %get-tuple-element.66._.refs_0_, bf16[16,3072]{1,0:T(8,128)(2,1)S(1)} %collective-permute-done.8.refs_1_, bf16[16,3072]{1,0:T(8,128)(2,1)S(1)} %collective-permute-done.9.refs_2_, ...), custom_call_target="tpu_custom_call" | custom-call | flops 3221225472 | tf_op jit(solution)/shard_map/pallas_call | solution.py:51
  58.1 3.0 %shard_map.145 = (f32[64,3072]{1,0:T(8,128)S(1)}, bf16[64,3072]{1,0:T(8,128)(2,1)S(1)}, bf16[3072,512]{1,0:T(8,128)(2,1)S(1)}, bf16[3072,512]{1,0:T(8,128)(2,1)S(1)}) custom-call(bf16[128,2048]{1,0:T(8,128)(2,1)S(1)} %get-tuple-element.74.hidden_ref, bf16[2048,3072]{1,0:T(8,128)(2,1)S(1)} %get-tuple-element.75.down_ref, bf16[2,3072,2048]{2,1,0:T(8,128)(2,1)} %refs_0_.2, ...), custom_call_target="tpu_custom_call" | custom-call | flops 1610612736 | tf_op jit(solution)/shard_map/pallas_call | solution.py:51
  61.1 0.6 collective-permute-start.23
  61.7 5.8 %shard_map.149 = (bf16[128,2048]{1,0:T(8,128)(2,1)S(1)}, bf16[3072,1536]{1,0:T(8,128)(2,1)S(1)}, bf16[2048,1024]{1,0:T(8,128)(2,1)S(1)}) custom-call(bf16[16,3072]{1,0:T(8,128)(2,1)S(1)} %get-tuple-element.66._.refs_0_, bf16[16,3072]{1,0:T(8,128)(2,1)S(1)} %collective-permute-done.8.refs_1_, bf16[16,3072]{1,0:T(8,128)(2,1)S(1)} %collective-permute-done.9.refs_2_, ...), custom_call_target="tpu_custom_call" | custom-call | flops 3221225472 | tf_op jit(solution)/shard_map/pallas_call | solution.py:51
  67.5 4.3 %shard_map.150 = (f32[64,3072]{1,0:T(8,128)S(1)}, bf16[64,3072]{1,0:T(8,128)(2,1)S(1)}, bf16[2048,2048]{1,0:T(8,128)(2,1)S(1)}) custom-call(bf16[128,2048]{1,0:T(8,128)(2,1)S(1)} %get-tuple-element.87.hidden_ref, bf16[2048,1024]{1,0:T(8,128)(2,1)S(1)} %get-tuple-element.88.down_ref, bf16[2,2048,3072]{2,1,0:T(8,128)(2,1)} %refs_0_.3, ...), custom_call_target="tpu_custom_call" | custom-call | flops 1610612736 | tf_op jit(solution)/shard_map/pallas_call | solution.py:51
  71.8 0.1 collective-permute-start.29
  71.9 1.1 %collective-permute-start.24 = (bf16[16,3072]{1,0:T(8,128)(2,1)S(1)}, bf16[16,3072]{1,0:T(8,128)(2,1)S(1)}, u32[]{:S(2)}, u32[]{:S(2)}) collective-permute-start(bf16[16,3072]{1,0:T(8,128)(2,1)S(1)} %get-tuple-element.78), channel_id=1, source_target_pairs={{0,2},{1,3},{2,0},{3,1},{4,6},{5,7},{6,4},{7,5},{8,10},{9,11},{10,... | collective-permute-start | bytes 294920 | tf_op jit(solution)/shard_map/ppermute | solution.py:458
  73.0 1.0 %collective-permute-start.26 = (bf16[16,3072]{1,0:T(8,128)(2,1)S(1)}, bf16[16,3072]{1,0:T(8,128)(2,1)S(1)}, u32[]{:S(2)}, u32[]{:S(2)}) collective-permute-start(bf16[16,3072]{1,0:T(8,128)(2,1)S(1)} %get-tuple-element.81.refs_2_), channel_id=1, source_target_pairs={{0,2},{1,3},{2,0},{3,1},{4,6},{5,7},{6,4},{7,5},{8,10},{9,11},{10,... | collective-permute-start | bytes 294920 | tf_op jit(solution)/shard_map/ppermute | solution.py:458
  74.0 1.1 %collective-permute-start.30 = (bf16[16,3072]{1,0:T(8,128)(2,1)S(1)}, bf16[16,3072]{1,0:T(8,128)(2,1)S(1)}, u32[]{:S(2)}, u32[]{:S(2)}) collective-permute-start(bf16[16,3072]{1,0:T(8,128)(2,1)S(1)} %get-tuple-element.92), channel_id=1, source_target_pairs={{0,2},{1,3},{2,0},{3,1},{4,6},{5,7},{6,4},{7,5},{8,10},{9,11},{10,... | collective-permute-start | bytes 294920 | tf_op jit(solution)/shard_map/ppermute | solution.py:458
  75.2 1.0 %collective-permute-start.32 = (bf16[16,3072]{1,0:T(8,128)(2,1)S(1)}, bf16[16,3072]{1,0:T(8,128)(2,1)S(1)}, u32[]{:S(2)}, u32[]{:S(2)}) collective-permute-start(bf16[16,3072]{1,0:T(8,128)(2,1)S(1)} %get-tuple-element.96), channel_id=1, source_target_pairs={{0,2},{1,3},{2,0},{3,1},{4,6},{5,7},{6,4},{7,5},{8,10},{9,11},{10,... | collective-permute-start | bytes 294920 | tf_op jit(solution)/shard_map/ppermute | solution.py:458
  76.1 1.5 %collective-permute-done.24.refs_2_ = bf16[16,3072]{1,0:T(8,128)(2,1)S(1)} collective-permute-done((bf16[16,3072]{1,0:T(8,128)(2,1)S(1)}, bf16[16,3072]{1,0:T(8,128)(2,1)S(1)}, u32[]{:S(2)}, u32[]{:S(2)}) %collective-permute-start.24) | collective-permute-done | bytes 98336 | tf_op jit(solution)/shard_map/ppermute | solution.py:458
  77.7 0.2 collective-permute-start.25
  77.8 1.9 %collective-permute-done.26.refs_2_ = bf16[16,3072]{1,0:T(8,128)(2,1)S(1)} collective-permute-done((bf16[16,3072]{1,0:T(8,128)(2,1)S(1)}, bf16[16,3072]{1,0:T(8,128)(2,1)S(1)}, u32[]{:S(2)}, u32[]{:S(2)}) %collective-permute-start.26) | collective-permute-done | bytes 98336 | tf_op jit(solution)/shard_map/ppermute | solution.py:458
  79.8 1.2 %collective-permute-start.27 = (bf16[8,3072]{1,0:T(8,128)(2,1)S(1)}, bf16[8,3072]{1,0:T(8,128)(2,1)S(1)}, u32[]{:S(2)}, u32[]{:S(2)}) collective-permute-start(bf16[8,3072]{1,0:T(8,128)(2,1)S(1)} %get-tuple-element.82), channel_id=1, source_target_pairs={{0,8},{4,12},{8,0},{12,4},{1,9},{5,13},{9,1},{13,5},{2,10},{6,14},... | collective-permute-start | bytes 147464 | tf_op jit(solution)/shard_map/ppermute | solution.py:458
  81.0 1.4 %collective-permute-start.28 = (bf16[8,3072]{1,0:T(8,128)(2,1)S(1)}, bf16[8,3072]{1,0:T(8,128)(2,1)S(1)}, u32[]{:S(2)}, u32[]{:S(2)}) collective-permute-start(bf16[8,3072]{1,0:T(8,128)(2,1)S(1)} %get-tuple-element.83), channel_id=1, source_target_pairs={{0,12},{4,8},{8,4},{12,0},{1,13},{5,9},{9,5},{13,1},{2,14},{6,10},... | collective-permute-start | bytes 147464 | tf_op jit(solution)/shard_map/ppermute | solution.py:458
  82.4 1.0 %collective-permute-start.31 = (bf16[8,3072]{1,0:T(8,128)(2,1)S(1)}, bf16[8,3072]{1,0:T(8,128)(2,1)S(1)}, u32[]{:S(2)}, u32[]{:S(2)}) collective-permute-start(bf16[8,3072]{1,0:T(8,128)(2,1)S(1)} %get-tuple-element.95), channel_id=1, source_target_pairs={{0,4},{4,0},{8,12},{12,8},{1,5},{5,1},{9,13},{13,9},{2,6},{6,2},{1... | collective-permute-start | bytes 147464 | tf_op jit(solution)/shard_map/ppermute | solution.py:458
  83.5 2.1 %collective-permute-start.33 = (bf16[8,3072]{1,0:T(8,128)(2,1)S(1)}, bf16[8,3072]{1,0:T(8,128)(2,1)S(1)}, u32[]{:S(2)}, u32[]{:S(2)}) collective-permute-start(bf16[8,3072]{1,0:T(8,128)(2,1)S(1)} %get-tuple-element.97), channel_id=1, source_target_pairs={{0,8},{4,12},{8,0},{12,4},{1,9},{5,13},{9,1},{13,5},{2,10},{6,14},... | collective-permute-start | bytes 147464 | tf_op jit(solution)/shard_map/ppermute | solution.py:458
  85.6 1.4 %collective-permute-start.34 = (bf16[8,3072]{1,0:T(8,128)(2,1)S(1)}, bf16[8,3072]{1,0:T(8,128)(2,1)S(1)}, u32[]{:S(2)}, u32[]{:S(2)}) collective-permute-start(bf16[8,3072]{1,0:T(8,128)(2,1)S(1)} %get-tuple-element.98), channel_id=1, source_target_pairs={{0,12},{4,8},{8,4},{12,0},{1,13},{5,9},{9,5},{13,1},{2,14},{6,10},... | collective-permute-start | bytes 147464 | tf_op jit(solution)/shard_map/ppermute | solution.py:458
  87.0 0.4 collective-permute-done.28.refs_3_
  87.4 2.7 %collective-permute-done.33.refs_6_ = bf16[8,3072]{1,0:T(8,128)(2,1)S(1)} collective-permute-done((bf16[8,3072]{1,0:T(8,128)(2,1)S(1)}, bf16[8,3072]{1,0:T(8,128)(2,1)S(1)}, u32[]{:S(2)}, u32[]{:S(2)}) %collective-permute-start.33) | collective-permute-done | bytes 49184 | tf_op jit(solution)/shard_map/ppermute | solution.py:458
  90.1 1.4 %collective-permute-done.34.refs_7_ = bf16[8,3072]{1,0:T(8,128)(2,1)S(1)} collective-permute-done((bf16[8,3072]{1,0:T(8,128)(2,1)S(1)}, bf16[8,3072]{1,0:T(8,128)(2,1)S(1)}, u32[]{:S(2)}, u32[]{:S(2)}) %collective-permute-start.34) | collective-permute-done | bytes 49184 | tf_op jit(solution)/shard_map/ppermute | solution.py:458
  91.5 0.9 %mix.1 = bf16[24,3072]{1,0:T(8,128)(2,1)} custom-call(f32[24,3072]{1,0:T(8,128)S(1)} %get-tuple-element.64.residual_ref, f32[24,64]{1,0:T(8,128)S(1)} %get-tuple-element.65.map_ref, bf16[8,3072]{1,0:T(8,128)(2,1)S(1)} %get-tuple-element.79.refs_0_, bf16[8,3072]{1,0:T(8,128)(2,1)S(1)} %collective-permute-done.25.refs_1_, ...), custom_call_target="tpu_custom_call" | custom-call | tf_op jit(solution)/shard_map/mix/pallas_call | solution.py:697
  (33 shorter events, 0.3 us)
Async XLA Ops:
  1.1 12.6 %collective-permute-start = (bf16[256,256]{1,0:T(8,128)(2,1)S(1)}, bf16[256,256]{1,0:T(8,128)(2,1)S(1)}, u32[]{:S(2)}, u32[]{:S(2)}) collective-permute-start(bf16[256,256]{1,0:T(8,128)(2,1)S(1)} %get-tuple-element.53), channel_id=1, source_target_pairs={{0,1},{1,0},{2,3},{3,2},{4,5},{5,4},{6,7},{7,6},{8,9},{9,8},{10,11... | collective-permute-start | bytes 393224 | tf_op jit(solution)/shard_map/ppermute | solution.py:526
  1.7 12.1 %collective-permute-start.1 = (bf16[256,256]{1,0:T(8,128)(2,1)S(1)}, bf16[256,256]{1,0:T(8,128)(2,1)S(1)}, u32[]{:S(2)}, u32[]{:S(2)}) collective-permute-start(bf16[256,256]{1,0:T(8,128)(2,1)S(1)} %get-tuple-element.54), channel_id=1, source_target_pairs={{0,2},{1,3},{2,0},{3,1},{4,6},{5,7},{6,4},{7,5},{8,10},{9,11},{10,... | collective-permute-start | bytes 393224 | tf_op jit(solution)/shard_map/ppermute | solution.py:526
  4.3 9.5 %collective-permute-start.2 = (bf16[256,256]{1,0:T(8,128)(2,1)S(1)}, bf16[256,256]{1,0:T(8,128)(2,1)S(1)}, u32[]{:S(2)}, u32[]{:S(2)}) collective-permute-start(bf16[256,256]{1,0:T(8,128)(2,1)S(1)} %get-tuple-element.55), channel_id=1, source_target_pairs={{0,3},{1,2},{2,1},{3,0},{4,7},{5,6},{6,5},{7,4},{8,11},{9,10},{10,... | collective-permute-start | bytes 393224 | tf_op jit(solution)/shard_map/ppermute | solution.py:526
  8.4 2.2 %collective-permute-start.3 = (bf16[48,128]{1,0:T(8,128)(2,1)S(1)}, bf16[48,128]{1,0:T(8,128)(2,1)S(1)}, u32[]{:S(2)}, u32[]{:S(2)}) collective-permute-start(bf16[48,128]{1,0:T(8,128)(2,1)S(1)} %get-tuple-element.57), channel_id=1, source_target_pairs={{0,1},{1,0},{2,3},{3,2},{4,5},{5,4},{6,7},{7,6},{8,9},{9,8},{10,11... | collective-permute-start | bytes 36872 | tf_op jit(solution)/shard_map/ppermute | solution.py:547
  8.6 3.7 %collective-permute-start.4 = (bf16[48,128]{1,0:T(8,128)(2,1)S(1)}, bf16[48,128]{1,0:T(8,128)(2,1)S(1)}, u32[]{:S(2)}, u32[]{:S(2)}) collective-permute-start(bf16[48,128]{1,0:T(8,128)(2,1)S(1)} %get-tuple-element.58), channel_id=1, source_target_pairs={{0,2},{1,3},{2,0},{3,1},{4,6},{5,7},{6,4},{7,5},{8,10},{9,11},{10,... | collective-permute-start | bytes 36872 | tf_op jit(solution)/shard_map/ppermute | solution.py:547
  10.6 3.2 %collective-permute-start.5 = (bf16[48,128]{1,0:T(8,128)(2,1)S(1)}, bf16[48,128]{1,0:T(8,128)(2,1)S(1)}, u32[]{:S(2)}, u32[]{:S(2)}) collective-permute-start(bf16[48,128]{1,0:T(8,128)(2,1)S(1)} %get-tuple-element.59), channel_id=1, source_target_pairs={{0,3},{1,2},{2,1},{3,0},{4,7},{5,6},{6,5},{7,4},{8,11},{9,10},{10,... | collective-permute-start | bytes 36872 | tf_op jit(solution)/shard_map/ppermute | solution.py:547
  18.4 1.6 %collective-permute-start.6 = (bf16[48,3072]{1,0:T(8,128)(2,1)S(1)}, bf16[48,3072]{1,0:T(8,128)(2,1)S(1)}, u32[]{:S(2)}, u32[]{:S(2)}) collective-permute-start(bf16[48,3072]{1,0:T(8,128)(2,1)S(1)} %get-tuple-element.62), channel_id=1, source_target_pairs={{0,1},{1,0},{2,3},{3,2},{4,5},{5,4},{6,7},{7,6},{8,9},{9,8},{10,11... | collective-permute-start | bytes 884744 | tf_op jit(solution)/shard_map/ppermute | solution.py:458
  20.1 6.0 %copy-start = (bf16[24,3072]{1,0:T(8,128)(2,1)S(1)}, bf16[24,3072]{1,0:T(8,128)(2,1)}, u32[]{:S(2)}) copy-start(bf16[24,3072]{1,0:T(8,128)(2,1)} %refs_3_.1) | copy-start | bytes 442372
  20.1 6.0 %copy-start.1 = (bf16[3072,8]{0,1:T(8,128)(2,1)S(1)}, bf16[3072,8]{0,1:T(8,128)(2,1)}, u32[]{:S(2)}) copy-start(bf16[3072,8]{0,1:T(8,128)(2,1)} %param.23) | copy-start | bytes 147460
  20.1 6.0 %copy-start.2 = (f32[3072]{0:T(1024)S(1)}, f32[3072]{0:T(1024)}, u32[]{:S(2)}) copy-start(f32[3072]{0:T(1024)} %param.22) | copy-start | bytes 36868
  20.1 6.0 %copy-start.3 = (s32[24,2]{0,1:T(2,128)S(1)}, s32[24,2]{0,1:T(2,128)}, u32[]{:S(2)}) copy-start(s32[24,2]{0,1:T(2,128)} %param.24) | copy-start | bytes 580
  20.1 6.0 %collective-permute-start.7 = (bf16[24,3072]{1,0:T(8,128)(2,1)S(1)}, bf16[24,3072]{1,0:T(8,128)(2,1)S(1)}, u32[]{:S(2)}, u32[]{:S(2)}) collective-permute-start(bf16[24,3072]{1,0:T(8,128)(2,1)S(1)} %shard_map.139._), channel_id=1, source_target_pairs={{0,2},{1,3},{2,0},{3,1},{4,6},{5,7},{6,4},{7,5},{8,10},{9,11},{10,... | collective-permute-start | bytes 442376 | tf_op jit(solution)/shard_map/ppermute | solution.py:458
  26.6 5.7 %collective-permute-start.8 = (bf16[16,3072]{1,0:T(8,128)(2,1)S(1)}, bf16[16,3072]{1,0:T(8,128)(2,1)S(1)}, u32[]{:S(2)}, u32[]{:S(2)}) collective-permute-start(bf16[16,3072]{1,0:T(8,128)(2,1)S(1)} %get-tuple-element.67), channel_id=1, source_target_pairs={{0,4},{4,0},{8,12},{12,8},{1,5},{5,1},{9,13},{13,9},{2,6},{6,2},{1... | collective-permute-start | bytes 294920 | tf_op jit(solution)/shard_map/ppermute | solution.py:458
  28.3 10.1 %collective-permute-start.9 = (bf16[16,3072]{1,0:T(8,128)(2,1)S(1)}, bf16[16,3072]{1,0:T(8,128)(2,1)S(1)}, u32[]{:S(2)}, u32[]{:S(2)}) collective-permute-start(bf16[16,3072]{1,0:T(8,128)(2,1)S(1)} %get-tuple-element.68), channel_id=1, source_target_pairs={{0,8},{4,12},{8,0},{12,4},{1,9},{5,13},{9,1},{13,5},{2,10},{6,14},... | collective-permute-start | bytes 294920 | tf_op jit(solution)/shard_map/ppermute | solution.py:458
  30.9 8.6 %collective-permute-start.10 = (bf16[16,3072]{1,0:T(8,128)(2,1)S(1)}, bf16[16,3072]{1,0:T(8,128)(2,1)S(1)}, u32[]{:S(2)}, u32[]{:S(2)}) collective-permute-start(bf16[16,3072]{1,0:T(8,128)(2,1)S(1)} %get-tuple-element.69), channel_id=1, source_target_pairs={{0,12},{4,8},{8,4},{12,0},{1,13},{5,9},{9,5},{13,1},{2,14},{6,10},... | collective-permute-start | bytes 294920 | tf_op jit(solution)/shard_map/ppermute | solution.py:458
  31.1 8.4 %collective-permute-start.15 = (bf16[16,3072]{1,0:T(8,128)(2,1)S(1)}, bf16[16,3072]{1,0:T(8,128)(2,1)S(1)}, u32[]{:S(2)}, u32[]{:S(2)}) collective-permute-start(bf16[16,3072]{1,0:T(8,128)(2,1)S(1)} %get-tuple-element.66._.refs_0_), channel_id=1, source_target_pairs={{0,1},{1,0},{2,3},{3,2},{4,5},{5,4},{6,7},{7,6},{8,9},{9,8},{10,11... | collective-permute-start | bytes 294920 | tf_op jit(solution)/shard_map/ppermute | solution.py:458
  31.1 9.4 %collective-permute-start.11 = (bf16[16,3072]{1,0:T(8,128)(2,1)S(1)}, bf16[16,3072]{1,0:T(8,128)(2,1)S(1)}, u32[]{:S(2)}, u32[]{:S(2)}) collective-permute-start(bf16[16,3072]{1,0:T(8,128)(2,1)S(1)} %get-tuple-element.66._.refs_0_), channel_id=1, source_target_pairs={{0,2},{1,3},{2,0},{3,1},{4,6},{5,7},{6,4},{7,5},{8,10},{9,11},{10,... | collective-permute-start | bytes 294920 | tf_op jit(solution)/shard_map/ppermute | solution.py:458
  32.3 9.3 %collective-permute-start.16 = (bf16[16,3072]{1,0:T(8,128)(2,1)S(1)}, bf16[16,3072]{1,0:T(8,128)(2,1)S(1)}, u32[]{:S(2)}, u32[]{:S(2)}) collective-permute-start(bf16[16,3072]{1,0:T(8,128)(2,1)S(1)} %collective-permute-done.8.refs_1_), channel_id=1, source_target_pairs={{0,1},{1,0},{2,3},{3,2},{4,5},{5,4},{6,7},{7,6},{8,9},{9,8},{10,11... | collective-permute-start | bytes 294920 | tf_op jit(solution)/shard_map/ppermute | solution.py:458
  38.4 5.1 %collective-permute-start.12 = (bf16[16,3072]{1,0:T(8,128)(2,1)S(1)}, bf16[16,3072]{1,0:T(8,128)(2,1)S(1)}, u32[]{:S(2)}, u32[]{:S(2)}) collective-permute-start(bf16[16,3072]{1,0:T(8,128)(2,1)S(1)} %collective-permute-done.8.refs_1_), channel_id=1, source_target_pairs={{0,2},{1,3},{2,0},{3,1},{4,6},{5,7},{6,4},{7,5},{8,10},{9,11},{10,... | collective-permute-start | bytes 294920 | tf_op jit(solution)/shard_map/ppermute | solution.py:458
  39.5 4.0 %collective-permute-start.17 = (bf16[16,3072]{1,0:T(8,128)(2,1)S(1)}, bf16[16,3072]{1,0:T(8,128)(2,1)S(1)}, u32[]{:S(2)}, u32[]{:S(2)}) collective-permute-start(bf16[16,3072]{1,0:T(8,128)(2,1)S(1)} %collective-permute-done.9.refs_2_), channel_id=1, source_target_pairs={{0,1},{1,0},{2,3},{3,2},{4,5},{5,4},{6,7},{7,6},{8,9},{9,8},{10,11... | collective-permute-start | bytes 294920 | tf_op jit(solution)/shard_map/ppermute | solution.py:458
  39.5 6.1 %collective-permute-start.13 = (bf16[16,3072]{1,0:T(8,128)(2,1)S(1)}, bf16[16,3072]{1,0:T(8,128)(2,1)S(1)}, u32[]{:S(2)}, u32[]{:S(2)}) collective-permute-start(bf16[16,3072]{1,0:T(8,128)(2,1)S(1)} %collective-permute-done.9.refs_2_), channel_id=1, source_target_pairs={{0,2},{1,3},{2,0},{3,1},{4,6},{5,7},{6,4},{7,5},{8,10},{9,11},{10,... | collective-permute-start | bytes 294920 | tf_op jit(solution)/shard_map/ppermute | solution.py:458
  40.5 6.7 %collective-permute-start.14 = (bf16[16,3072]{1,0:T(8,128)(2,1)S(1)}, bf16[16,3072]{1,0:T(8,128)(2,1)S(1)}, u32[]{:S(2)}, u32[]{:S(2)}) collective-permute-start(bf16[16,3072]{1,0:T(8,128)(2,1)S(1)} %collective-permute-done.10.refs_3_), channel_id=1, source_target_pairs={{0,2},{1,3},{2,0},{3,1},{4,6},{5,7},{6,4},{7,5},{8,10},{9,11},{10,... | collective-permute-start | bytes 294920 | tf_op jit(solution)/shard_map/ppermute | solution.py:458
  41.6 11.9 %collective-permute-start.18 = (bf16[16,3072]{1,0:T(8,128)(2,1)S(1)}, bf16[16,3072]{1,0:T(8,128)(2,1)S(1)}, u32[]{:S(2)}, u32[]{:S(2)}) collective-permute-start(bf16[16,3072]{1,0:T(8,128)(2,1)S(1)} %collective-permute-done.10.refs_3_), channel_id=1, source_target_pairs={{0,1},{1,0},{2,3},{3,2},{4,5},{5,4},{6,7},{7,6},{8,9},{9,8},{10,11... | collective-permute-start | bytes 294920 | tf_op jit(solution)/shard_map/ppermute | solution.py:458
  43.5 10.0 %collective-permute-start.19 = (bf16[16,3072]{1,0:T(8,128)(2,1)S(1)}, bf16[16,3072]{1,0:T(8,128)(2,1)S(1)}, u32[]{:S(2)}, u32[]{:S(2)}) collective-permute-start(bf16[16,3072]{1,0:T(8,128)(2,1)S(1)} %collective-permute-done.11.refs_4_), channel_id=1, source_target_pairs={{0,1},{1,0},{2,3},{3,2},{4,5},{5,4},{6,7},{7,6},{8,9},{9,8},{10,11... | collective-permute-start | bytes 294920 | tf_op jit(solution)/shard_map/ppermute | solution.py:458
  43.5 10.0 %collective-permute-start.20 = (bf16[16,3072]{1,0:T(8,128)(2,1)S(1)}, bf16[16,3072]{1,0:T(8,128)(2,1)S(1)}, u32[]{:S(2)}, u32[]{:S(2)}) collective-permute-start(bf16[16,3072]{1,0:T(8,128)(2,1)S(1)} %collective-permute-done.12.refs_5_), channel_id=1, source_target_pairs={{0,1},{1,0},{2,3},{3,2},{4,5},{5,4},{6,7},{7,6},{8,9},{9,8},{10,11... | collective-permute-start | bytes 294920 | tf_op jit(solution)/shard_map/ppermute | solution.py:458
  45.6 7.9 %collective-permute-start.21 = (bf16[16,3072]{1,0:T(8,128)(2,1)S(1)}, bf16[16,3072]{1,0:T(8,128)(2,1)S(1)}, u32[]{:S(2)}, u32[]{:S(2)}) collective-permute-start(bf16[16,3072]{1,0:T(8,128)(2,1)S(1)} %collective-permute-done.13.refs_6_), channel_id=1, source_target_pairs={{0,1},{1,0},{2,3},{3,2},{4,5},{5,4},{6,7},{7,6},{8,9},{9,8},{10,11... | collective-permute-start | bytes 294920 | tf_op jit(solution)/shard_map/ppermute | solution.py:458
  47.3 6.2 %collective-permute-start.22 = (bf16[16,3072]{1,0:T(8,128)(2,1)S(1)}, bf16[16,3072]{1,0:T(8,128)(2,1)S(1)}, u32[]{:S(2)}, u32[]{:S(2)}) collective-permute-start(bf16[16,3072]{1,0:T(8,128)(2,1)S(1)} %collective-permute-done.14.refs_7_), channel_id=1, source_target_pairs={{0,1},{1,0},{2,3},{3,2},{4,5},{5,4},{6,7},{7,6},{8,9},{9,8},{10,11... | collective-permute-start | bytes 294920 | tf_op jit(solution)/shard_map/ppermute | solution.py:458
  61.1 6.3 %collective-permute-start.23 = (bf16[64,3072]{1,0:T(8,128)(2,1)S(1)}, bf16[64,3072]{1,0:T(8,128)(2,1)S(1)}, u32[]{:S(2)}, u32[]{:S(2)}) collective-permute-start(bf16[64,3072]{1,0:T(8,128)(2,1)S(1)} %get-tuple-element.77), channel_id=1, source_target_pairs={{0,1},{1,0},{2,3},{3,2},{4,5},{5,4},{6,7},{7,6},{8,9},{9,8},{10,11... | collective-permute-start | bytes 1179656 | tf_op jit(solution)/shard_map/ppermute | solution.py:458
  71.8 2.2 %collective-permute-start.29 = (bf16[64,3072]{1,0:T(8,128)(2,1)S(1)}, bf16[64,3072]{1,0:T(8,128)(2,1)S(1)}, u32[]{:S(2)}, u32[]{:S(2)}) collective-permute-start(bf16[64,3072]{1,0:T(8,128)(2,1)S(1)} %get-tuple-element.91), channel_id=1, source_target_pairs={{0,1},{1,0},{2,3},{3,2},{4,5},{5,4},{6,7},{7,6},{8,9},{9,8},{10,11... | collective-permute-start | bytes 1179656 | tf_op jit(solution)/shard_map/ppermute | solution.py:458
  71.9 5.7 %collective-permute-start.24 = (bf16[16,3072]{1,0:T(8,128)(2,1)S(1)}, bf16[16,3072]{1,0:T(8,128)(2,1)S(1)}, u32[]{:S(2)}, u32[]{:S(2)}) collective-permute-start(bf16[16,3072]{1,0:T(8,128)(2,1)S(1)} %get-tuple-element.78), channel_id=1, source_target_pairs={{0,2},{1,3},{2,0},{3,1},{4,6},{5,7},{6,4},{7,5},{8,10},{9,11},{10,... | collective-permute-start | bytes 294920 | tf_op jit(solution)/shard_map/ppermute | solution.py:458
  73.0 6.7 %collective-permute-start.26 = (bf16[16,3072]{1,0:T(8,128)(2,1)S(1)}, bf16[16,3072]{1,0:T(8,128)(2,1)S(1)}, u32[]{:S(2)}, u32[]{:S(2)}) collective-permute-start(bf16[16,3072]{1,0:T(8,128)(2,1)S(1)} %get-tuple-element.81.refs_2_), channel_id=1, source_target_pairs={{0,2},{1,3},{2,0},{3,1},{4,6},{5,7},{6,4},{7,5},{8,10},{9,11},{10,... | collective-permute-start | bytes 294920 | tf_op jit(solution)/shard_map/ppermute | solution.py:458
  74.0 8.4 %collective-permute-start.30 = (bf16[16,3072]{1,0:T(8,128)(2,1)S(1)}, bf16[16,3072]{1,0:T(8,128)(2,1)S(1)}, u32[]{:S(2)}, u32[]{:S(2)}) collective-permute-start(bf16[16,3072]{1,0:T(8,128)(2,1)S(1)} %get-tuple-element.92), channel_id=1, source_target_pairs={{0,2},{1,3},{2,0},{3,1},{4,6},{5,7},{6,4},{7,5},{8,10},{9,11},{10,... | collective-permute-start | bytes 294920 | tf_op jit(solution)/shard_map/ppermute | solution.py:458
  75.2 8.3 %collective-permute-start.32 = (bf16[16,3072]{1,0:T(8,128)(2,1)S(1)}, bf16[16,3072]{1,0:T(8,128)(2,1)S(1)}, u32[]{:S(2)}, u32[]{:S(2)}) collective-permute-start(bf16[16,3072]{1,0:T(8,128)(2,1)S(1)} %get-tuple-element.96), channel_id=1, source_target_pairs={{0,2},{1,3},{2,0},{3,1},{4,6},{5,7},{6,4},{7,5},{8,10},{9,11},{10,... | collective-permute-start | bytes 294920 | tf_op jit(solution)/shard_map/ppermute | solution.py:458
  77.7 7.9 %collective-permute-start.25 = (bf16[8,3072]{1,0:T(8,128)(2,1)S(1)}, bf16[8,3072]{1,0:T(8,128)(2,1)S(1)}, u32[]{:S(2)}, u32[]{:S(2)}) collective-permute-start(bf16[8,3072]{1,0:T(8,128)(2,1)S(1)} %get-tuple-element.80), channel_id=1, source_target_pairs={{0,4},{4,0},{8,12},{12,8},{1,5},{5,1},{9,13},{13,9},{2,6},{6,2},{1... | collective-permute-start | bytes 147464 | tf_op jit(solution)/shard_map/ppermute | solution.py:458
  79.8 7.2 %collective-permute-start.27 = (bf16[8,3072]{1,0:T(8,128)(2,1)S(1)}, bf16[8,3072]{1,0:T(8,128)(2,1)S(1)}, u32[]{:S(2)}, u32[]{:S(2)}) collective-permute-start(bf16[8,3072]{1,0:T(8,128)(2,1)S(1)} %get-tuple-element.82), channel_id=1, source_target_pairs={{0,8},{4,12},{8,0},{12,4},{1,9},{5,13},{9,1},{13,5},{2,10},{6,14},... | collective-permute-start | bytes 147464 | tf_op jit(solution)/shard_map/ppermute | solution.py:458
  81.0 6.4 %collective-permute-start.28 = (bf16[8,3072]{1,0:T(8,128)(2,1)S(1)}, bf16[8,3072]{1,0:T(8,128)(2,1)S(1)}, u32[]{:S(2)}, u32[]{:S(2)}) collective-permute-start(bf16[8,3072]{1,0:T(8,128)(2,1)S(1)} %get-tuple-element.83), channel_id=1, source_target_pairs={{0,12},{4,8},{8,4},{12,0},{1,13},{5,9},{9,5},{13,1},{2,14},{6,10},... | collective-permute-start | bytes 147464 | tf_op jit(solution)/shard_map/ppermute | solution.py:458
  82.4 4.9 %collective-permute-start.31 = (bf16[8,3072]{1,0:T(8,128)(2,1)S(1)}, bf16[8,3072]{1,0:T(8,128)(2,1)S(1)}, u32[]{:S(2)}, u32[]{:S(2)}) collective-permute-start(bf16[8,3072]{1,0:T(8,128)(2,1)S(1)} %get-tuple-element.95), channel_id=1, source_target_pairs={{0,4},{4,0},{8,12},{12,8},{1,5},{5,1},{9,13},{13,9},{2,6},{6,2},{1... | collective-permute-start | bytes 147464 | tf_op jit(solution)/shard_map/ppermute | solution.py:458
  83.5 6.6 %collective-permute-start.33 = (bf16[8,3072]{1,0:T(8,128)(2,1)S(1)}, bf16[8,3072]{1,0:T(8,128)(2,1)S(1)}, u32[]{:S(2)}, u32[]{:S(2)}) collective-permute-start(bf16[8,3072]{1,0:T(8,128)(2,1)S(1)} %get-tuple-element.97), channel_id=1, source_target_pairs={{0,8},{4,12},{8,0},{12,4},{1,9},{5,13},{9,1},{13,5},{2,10},{6,14},... | collective-permute-start | bytes 147464 | tf_op jit(solution)/shard_map/ppermute | solution.py:458
  85.6 5.9 %collective-permute-start.34 = (bf16[8,3072]{1,0:T(8,128)(2,1)S(1)}, bf16[8,3072]{1,0:T(8,128)(2,1)S(1)}, u32[]{:S(2)}, u32[]{:S(2)}) collective-permute-start(bf16[8,3072]{1,0:T(8,128)(2,1)S(1)} %get-tuple-element.98), channel_id=1, source_target_pairs={{0,12},{4,8},{8,4},{12,0},{1,13},{5,9},{9,5},{13,1},{2,14},{6,10},... | collective-permute-start | bytes 147464 | tf_op jit(solution)/shard_map/ppermute | solution.py:458

commit v2 on v1

--- a/solution.py
+++ b/solution.py
@@ -337,12 +337,16 @@
         else:
             gate_tile = gate_refs[1][:, start - first_width : start - first_width + tile]
         gate = jnp.dot(x_all[...], gate_tile, preferred_element_type=F32)
-        gates[:, start : start + tile] = gate / (1.0 + jnp.exp(-gate))
-    for i in range(tiles):
+        gate = gate / (1.0 + jnp.exp(-gate))
+        if resident:
+            up_tile = up_ref[:, start : start + tile]
+            up = jnp.dot(x_all[...], up_tile, preferred_element_type=F32)
+            hidden_ref[:, start : start + tile] = (gate * up).astype(BF16)
+        else:
+            gates[:, start : start + tile] = gate
+    for i in range(0 if resident else tiles):
         cols = slice(i * tile, (i + 1) * tile)
-        if resident:
-            up_tile = up_ref[:, cols]
-        elif i == 0:
+        if i == 0:
             up_tile = up_low[...]
         else:
             copies[i - 1].wait()
@@ -388,14 +392,14 @@
                     sems.at[2 + i],
                 )
             )
-        for copy in copies[:3]:
+        for copy in copies[:4]:
             copy.start()
     for start in range(0, width, tile):
         cols = slice(start, start + tile)
         if start >= split:
             i = (start - split) // tile
             copies[i].wait()
-            for copy in copies[i + 3 : i + 4]:
+            for copy in copies[i + 4 : i + 5]:
                 copy.start()
             down_tile = rest_ref[:, i * tile : (i + 1) * tile]
         else:
@@ -595,10 +599,10 @@
         block = block + [send_to(b, "ten", bit) for b in block]
 
     hidden_units = w_gate.shape[2]
-    gate_half = hidden_units // 2
-    gate_a, gate_token = fetch(w_gate, 0, slots[0], gate_half)
-    gate_b, _ = fetch(w_gate, 0, gate_token, gate_half, gate_half)
     tile = min(512, hidden_units // 4)
+    gate_first = hidden_units - tile
+    gate_a, gate_token = fetch(w_gate, 0, slots[0], gate_first)
+    gate_b, _ = fetch(w_gate, 0, gate_token, tile, gate_first)
     tiles = hidden_units // tile
     down_low_width = 2 * tile
     half = len(block) * SLOTS // 2

time: 92.7 us -> 92.1 us (level)
  transfers between devices with their start and end apart: 35 -> 35, of which waited for: 14 -> 14; matrix products, arithmetic and copies ran while one was open for 0% -> 0% of each run, Pallas kernels for 22% -> 23%
where the time goes in v2:
time: 92.1 us; the launch traced here: 91.8 us
  Pallas kernels  39.3 us (43%)
  starting transfers between devices  28.4 us (31%)
  waiting for transfers between devices  23.2 us (25%)
    pallas_call x18, Pallas kernels, call(): pl.pallas_call(kernel, in_specs=specs, out_specs=[VMEM] * len(outs), out_...  38.4 us
    ppermute x29, starting transfers between devices, send_to(): return lax.ppermute(x, axis, xor_pairs(lax.axis_size(axis), distance))  22.2 us
    ppermute x29, waiting for transfers between devices, send_to(): return lax.ppermute(x, axis, xor_pairs(lax.axis_size(axis), distance))  21.4 us
    ppermute x3, starting transfers between devices, on_device(): lax.ppermute(packed[d], 'ten', xor_pairs(ten, d))  3.18 us
    ppermute x3, starting transfers between devices, on_device(): lax.ppermute(decoded[d], 'ten', xor_pairs(ten, d))  2.95 us
  transfers between devices with their start and end apart: 35, of which 14 were waited for; matrix products, arithmetic and copies ran while one was open for 0% of the time, Pallas kernels for 23%

profile of v2, /device:TPU:0, one launch (start us, length us, event | category | flops | bytes accessed | tf_op | source)
XLA Modules:
  0.0 91.8 jit_solution(6388626216414984517)
XLA Ops:
  0.0 1.1 %shard_map.136 = (bf16[256,256]{1,0:T(8,128)(2,1)S(1)}, bf16[256,256]{1,0:T(8,128)(2,1)S(1)}, bf16[256,256]{1,0:T(8,128)(2,1)S(1)}, bf16[256,256]{1,0:T(8,128)(2,1)S(1)}) custom-call(bf16[24,6144]{1,0:T(8,128)(2,1)} %q_hbm.3, bf16[2,24,1024]{2,1,0:T(8,128)(2,1)} %new_hbm.3, bf16[2,1,32,1024]{3,2,1,0:T(8,128)(2,1)} %prefix_hbm.1), custom_call_target="tpu_custom_call" | custom-call | tf_op jit(solution)/shard_map/pallas_call | solution.py:51
  1.1 0.6 collective-permute-start
  1.7 2.6 %collective-permute-start.1 = (bf16[256,256]{1,0:T(8,128)(2,1)S(1)}, bf16[256,256]{1,0:T(8,128)(2,1)S(1)}, u32[]{:S(2)}, u32[]{:S(2)}) collective-permute-start(bf16[256,256]{1,0:T(8,128)(2,1)S(1)} %get-tuple-element.54), channel_id=1, source_target_pairs={{0,2},{1,3},{2,0},{3,1},{4,6},{5,7},{6,4},{7,5},{8,10},{9,11},{10,... | collective-permute-start | bytes 393224 | tf_op jit(solution)/shard_map/ppermute | solution.py:530
  4.3 0.0 collective-permute-start.2
  4.3 4.1 %shard_map.137 = (bf16[48,128]{1,0:T(8,128)(2,1)S(1)}, bf16[48,128]{1,0:T(8,128)(2,1)S(1)}, bf16[48,128]{1,0:T(8,128)(2,1)S(1)}, bf16[48,128]{1,0:T(8,128)(2,1)S(1)}, bf16[1536,3072]{1,0:T(8,128)(2,1)S(1)}) custom-call(s32[4]{0:T(128)} %len_hbm.1, bf16[24,6144]{1,0:T(8,128)(2,1)} %q_hbm.3, bf16[2,4,48,1024]{3,2,1,0:T(8,128)(2,1)} %kv_hbm.1, ...), custom_call_target="tpu_custom_call" | custom-call | tf_op jit(solution)/shard_map/pallas_call | solution.py:51
  8.4 0.2 collective-permute-start.3
  8.6 1.9 %collective-permute-start.4 = (bf16[48,128]{1,0:T(8,128)(2,1)S(1)}, bf16[48,128]{1,0:T(8,128)(2,1)S(1)}, u32[]{:S(2)}, u32[]{:S(2)}) collective-permute-start(bf16[48,128]{1,0:T(8,128)(2,1)S(1)} %get-tuple-element.58), channel_id=1, source_target_pairs={{0,2},{1,3},{2,0},{3,1},{4,6},{5,7},{6,4},{7,5},{8,10},{9,11},{10,... | collective-permute-start | bytes 36872 | tf_op jit(solution)/shard_map/ppermute | solution.py:551
  10.6 0.8 collective-permute-start.5
  12.0 0.3 collective-permute-done.4.refs_6_
  12.3 1.5 %collective-permute-done.5.refs_7_ = bf16[48,128]{1,0:T(8,128)(2,1)S(1)} collective-permute-done((bf16[48,128]{1,0:T(8,128)(2,1)S(1)}, bf16[48,128]{1,0:T(8,128)(2,1)S(1)}, u32[]{:S(2)}, u32[]{:S(2)}) %collective-permute-start.5) | collective-permute-done | bytes 12320 | tf_op jit(solution)/shard_map/ppermute | solution.py:551
  13.8 0.0 collective-permute-done.refs_1_
  13.8 0.0 collective-permute-done.1.refs_2_
  13.8 0.0 collective-permute-done.2.refs_3_
  13.8 4.6 %shard_map.138 = (f32[48,3072]{1,0:T(8,128)S(1)}, bf16[48,3072]{1,0:T(8,128)(2,1)S(1)}, bf16[3072,2048]{1,0:T(8,128)(2,1)S(1)}) custom-call(s32[1]{0:T(128)S(6)} %copy.15.len_ref, bf16[256,256]{1,0:T(8,128)(2,1)S(1)} %get-tuple-element.52.refs_0_, bf16[256,256]{1,0:T(8,128)(2,1)S(1)} %collective-permute-done.refs_1_, ...), custom_call_target="tpu_custom_call" | custom-call | tf_op jit(solution)/shard_map/pallas_call | solution.py:51
  18.4 0.2 collective-permute-start.6
  18.6 1.5 %collective-permute-done.6.refs_1_ = bf16[48,3072]{1,0:T(8,128)(2,1)S(1)} collective-permute-done((bf16[48,3072]{1,0:T(8,128)(2,1)S(1)}, bf16[48,3072]{1,0:T(8,128)(2,1)S(1)}, u32[]{:S(2)}, u32[]{:S(2)}) %collective-permute-start.6) | collective-permute-done | bytes 294944 | tf_op jit(solution)/shard_map/ppermute | solution.py:462
  20.1 0.0 copy-start
  20.1 0.0 copy-start.1
  20.1 0.0 copy-start.2
  20.1 0.0 copy-start.3
  20.1 0.8 collective-permute-start.7
  20.9 4.6 %shard_map.140 = (bf16[2048,3072]{1,0:T(8,128)(2,1)S(1)}, f32[8,128]{1,0:T(8,128)S(1)}) custom-call(bf16[2,2048,3072]{2,1,0:T(8,128)(2,1)} %refs_0_.3, bf16[24,3072]{1,0:T(8,128)(2,1)S(1)} %shard_map.139._), custom_call_target="tpu_custom_call" | custom-call | tf_op jit(solution)/shard_map/pallas_call | solution.py:51
  25.5 0.5 collective-permute-done.7.refs_2_
  26.1 0.6 shard_map.141
  26.6 1.6 %collective-permute-start.8 = (bf16[16,3072]{1,0:T(8,128)(2,1)S(1)}, bf16[16,3072]{1,0:T(8,128)(2,1)S(1)}, u32[]{:S(2)}, u32[]{:S(2)}) collective-permute-start(bf16[16,3072]{1,0:T(8,128)(2,1)S(1)} %get-tuple-element.67), channel_id=1, source_target_pairs={{0,4},{4,0},{8,12},{12,8},{1,5},{5,1},{9,13},{13,9},{2,6},{6,2},{1... | collective-permute-start | bytes 294920 | tf_op jit(solution)/shard_map/ppermute | solution.py:462
  28.3 2.6 %collective-permute-start.9 = (bf16[16,3072]{1,0:T(8,128)(2,1)S(1)}, bf16[16,3072]{1,0:T(8,128)(2,1)S(1)}, u32[]{:S(2)}, u32[]{:S(2)}) collective-permute-start(bf16[16,3072]{1,0:T(8,128)(2,1)S(1)} %get-tuple-element.68), channel_id=1, source_target_pairs={{0,8},{4,12},{8,0},{12,4},{1,9},{5,13},{9,1},{13,5},{2,10},{6,14},... | collective-permute-start | bytes 294920 | tf_op jit(solution)/shard_map/ppermute | solution.py:462
  30.9 0.2 collective-permute-start.10
  31.1 1.0 %collective-permute-start.11 = (bf16[16,3072]{1,0:T(8,128)(2,1)S(1)}, bf16[16,3072]{1,0:T(8,128)(2,1)S(1)}, u32[]{:S(2)}, u32[]{:S(2)}) collective-permute-start(bf16[16,3072]{1,0:T(8,128)(2,1)S(1)} %get-tuple-element.66._.refs_0_), channel_id=1, source_target_pairs={{0,2},{1,3},{2,0},{3,1},{4,6},{5,7},{6,4},{7,5},{8,10},{9,11},{10,... | collective-permute-start | bytes 294920 | tf_op jit(solution)/shard_map/ppermute | solution.py:462
  32.1 0.2 collective-permute-done.8.refs_1_
  32.3 0.0 collective-permute-start.16
  32.3 6.1 %collective-permute-done.9.refs_2_ = bf16[16,3072]{1,0:T(8,128)(2,1)S(1)} collective-permute-done((bf16[16,3072]{1,0:T(8,128)(2,1)S(1)}, bf16[16,3072]{1,0:T(8,128)(2,1)S(1)}, u32[]{:S(2)}, u32[]{:S(2)}) %collective-permute-start.9) | collective-permute-done | bytes 98336 | tf_op jit(solution)/shard_map/ppermute | solution.py:462
  38.4 1.1 %collective-permute-start.12 = (bf16[16,3072]{1,0:T(8,128)(2,1)S(1)}, bf16[16,3072]{1,0:T(8,128)(2,1)S(1)}, u32[]{:S(2)}, u32[]{:S(2)}) collective-permute-start(bf16[16,3072]{1,0:T(8,128)(2,1)S(1)} %collective-permute-done.8.refs_1_), channel_id=1, source_target_pairs={{0,2},{1,3},{2,0},{3,1},{4,6},{5,7},{6,4},{7,5},{8,10},{9,11},{10,... | collective-permute-start | bytes 294920 | tf_op jit(solution)/shard_map/ppermute | solution.py:462
  39.5 1.0 %collective-permute-start.13 = (bf16[16,3072]{1,0:T(8,128)(2,1)S(1)}, bf16[16,3072]{1,0:T(8,128)(2,1)S(1)}, u32[]{:S(2)}, u32[]{:S(2)}) collective-permute-start(bf16[16,3072]{1,0:T(8,128)(2,1)S(1)} %collective-permute-done.9.refs_2_), channel_id=1, source_target_pairs={{0,2},{1,3},{2,0},{3,1},{4,6},{5,7},{6,4},{7,5},{8,10},{9,11},{10,... | collective-permute-start | bytes 294920 | tf_op jit(solution)/shard_map/ppermute | solution.py:462
  40.5 0.0 collective-permute-done.11.refs_4_
  40.5 1.1 %collective-permute-start.14 = (bf16[16,3072]{1,0:T(8,128)(2,1)S(1)}, bf16[16,3072]{1,0:T(8,128)(2,1)S(1)}, u32[]{:S(2)}, u32[]{:S(2)}) collective-permute-start(bf16[16,3072]{1,0:T(8,128)(2,1)S(1)} %collective-permute-done.10.refs_3_), channel_id=1, source_target_pairs={{0,2},{1,3},{2,0},{3,1},{4,6},{5,7},{6,4},{7,5},{8,10},{9,11},{10,... | collective-permute-start | bytes 294920 | tf_op jit(solution)/shard_map/ppermute | solution.py:462
  41.6 0.0 collective-permute-start.18
  41.6 1.9 %collective-permute-done.12.refs_5_ = bf16[16,3072]{1,0:T(8,128)(2,1)S(1)} collective-permute-done((bf16[16,3072]{1,0:T(8,128)(2,1)S(1)}, bf16[16,3072]{1,0:T(8,128)(2,1)S(1)}, u32[]{:S(2)}, u32[]{:S(2)}) %collective-permute-start.12) | collective-permute-done | bytes 98336 | tf_op jit(solution)/shard_map/ppermute | solution.py:462
  43.5 0.5 collective-permute-start.20
  44.0 1.6 %collective-permute-done.13.refs_6_ = bf16[16,3072]{1,0:T(8,128)(2,1)S(1)} collective-permute-done((bf16[16,3072]{1,0:T(8,128)(2,1)S(1)}, bf16[16,3072]{1,0:T(8,128)(2,1)S(1)}, u32[]{:S(2)}, u32[]{:S(2)}) %collective-permute-start.13) | collective-permute-done | bytes 98336 | tf_op jit(solution)/shard_map/ppermute | solution.py:462
  45.6 1.7 %collective-permute-done.14.refs_7_ = bf16[16,3072]{1,0:T(8,128)(2,1)S(1)} collective-permute-done((bf16[16,3072]{1,0:T(8,128)(2,1)S(1)}, bf16[16,3072]{1,0:T(8,128)(2,1)S(1)}, u32[]{:S(2)}, u32[]{:S(2)}) %collective-permute-start.14) | collective-permute-done | bytes 98336 | tf_op jit(solution)/shard_map/ppermute | solution.py:462
  47.3 3.7 %shard_map.142 = (bf16[3072,1536]{1,0:T(8,128)(2,1)S(1)}, f32[8,128]{1,0:T(8,128)S(1)}) custom-call(bf16[2,3072,2048]{2,1,0:T(8,128)(2,1)} %refs_0_.2, bf16[16,3072]{1,0:T(8,128)(2,1)S(1)} %get-tuple-element.66._.refs_0_), custom_call_target="tpu_custom_call" | custom-call | tf_op jit(solution)/shard_map/pallas_call | solution.py:51
  51.0 2.5 %shard_map.143 = (bf16[3072,512]{1,0:T(8,128)(2,1)S(1)}, f32[8,128]{1,0:T(8,128)}) custom-call(bf16[2,3072,2048]{2,1,0:T(8,128)(2,1)} %refs_0_.2, f32[8,128]{1,0:T(8,128)S(1)} %get-tuple-element.71._), custom_call_target="tpu_custom_call" | custom-call | tf_op jit(solution)/shard_map/pallas_call | solution.py:51
  53.5 4.2 %shard_map.144 = (bf16[128,2048]{1,0:T(8,128)(2,1)S(1)}, bf16[3072,1536]{1,0:T(8,128)(2,1)S(1)}) custom-call(bf16[16,3072]{1,0:T(8,128)(2,1)S(1)} %get-tuple-element.66._.refs_0_, bf16[16,3072]{1,0:T(8,128)(2,1)S(1)} %collective-permute-done.8.refs_1_, bf16[16,3072]{1,0:T(8,128)(2,1)S(1)} %collective-permute-done.9.refs_2_, ...), custom_call_target="tpu_custom_call" | custom-call | flops 3221225472 | tf_op jit(solution)/shard_map/pallas_call | solution.py:51
  57.7 3.0 %shard_map.145 = (f32[64,3072]{1,0:T(8,128)S(1)}, bf16[64,3072]{1,0:T(8,128)(2,1)S(1)}, bf16[3072,512]{1,0:T(8,128)(2,1)S(1)}, bf16[3072,512]{1,0:T(8,128)(2,1)S(1)}) custom-call(bf16[128,2048]{1,0:T(8,128)(2,1)S(1)} %get-tuple-element.74.hidden_ref, bf16[2048,3072]{1,0:T(8,128)(2,1)S(1)} %get-tuple-element.75.down_ref, bf16[2,3072,2048]{2,1,0:T(8,128)(2,1)} %refs_0_.2, ...), custom_call_target="tpu_custom_call" | custom-call | flops 1610612736 | tf_op jit(solution)/shard_map/pallas_call | solution.py:51
  60.7 0.6 collective-permute-start.23
  61.3 5.8 %shard_map.149 = (bf16[128,2048]{1,0:T(8,128)(2,1)S(1)}, bf16[3072,1536]{1,0:T(8,128)(2,1)S(1)}, bf16[2048,1024]{1,0:T(8,128)(2,1)S(1)}) custom-call(bf16[16,3072]{1,0:T(8,128)(2,1)S(1)} %get-tuple-element.66._.refs_0_, bf16[16,3072]{1,0:T(8,128)(2,1)S(1)} %collective-permute-done.8.refs_1_, bf16[16,3072]{1,0:T(8,128)(2,1)S(1)} %collective-permute-done.9.refs_2_, ...), custom_call_target="tpu_custom_call" | custom-call | flops 3221225472 | tf_op jit(solution)/shard_map/pallas_call | solution.py:51
  67.1 4.1 %shard_map.150 = (f32[64,3072]{1,0:T(8,128)S(1)}, bf16[64,3072]{1,0:T(8,128)(2,1)S(1)}, bf16[2048,2048]{1,0:T(8,128)(2,1)S(1)}) custom-call(bf16[128,2048]{1,0:T(8,128)(2,1)S(1)} %get-tuple-element.87.hidden_ref, bf16[2048,1024]{1,0:T(8,128)(2,1)S(1)} %get-tuple-element.88.down_ref, bf16[2,2048,3072]{2,1,0:T(8,128)(2,1)} %refs_0_.3, ...), custom_call_target="tpu_custom_call" | custom-call | flops 1610612736 | tf_op jit(solution)/shard_map/pallas_call | solution.py:51
  71.2 0.1 collective-permute-start.29
  71.3 1.1 %collective-permute-start.24 = (bf16[16,3072]{1,0:T(8,128)(2,1)S(1)}, bf16[16,3072]{1,0:T(8,128)(2,1)S(1)}, u32[]{:S(2)}, u32[]{:S(2)}) collective-permute-start(bf16[16,3072]{1,0:T(8,128)(2,1)S(1)} %get-tuple-element.78), channel_id=1, source_target_pairs={{0,2},{1,3},{2,0},{3,1},{4,6},{5,7},{6,4},{7,5},{8,10},{9,11},{10,... | collective-permute-start | bytes 294920 | tf_op jit(solution)/shard_map/ppermute | solution.py:462
  72.4 1.0 %collective-permute-start.26 = (bf16[16,3072]{1,0:T(8,128)(2,1)S(1)}, bf16[16,3072]{1,0:T(8,128)(2,1)S(1)}, u32[]{:S(2)}, u32[]{:S(2)}) collective-permute-start(bf16[16,3072]{1,0:T(8,128)(2,1)S(1)} %get-tuple-element.81.refs_2_), channel_id=1, source_target_pairs={{0,2},{1,3},{2,0},{3,1},{4,6},{5,7},{6,4},{7,5},{8,10},{9,11},{10,... | collective-permute-start | bytes 294920 | tf_op jit(solution)/shard_map/ppermute | solution.py:462
  73.4 1.1 %collective-permute-start.30 = (bf16[16,3072]{1,0:T(8,128)(2,1)S(1)}, bf16[16,3072]{1,0:T(8,128)(2,1)S(1)}, u32[]{:S(2)}, u32[]{:S(2)}) collective-permute-start(bf16[16,3072]{1,0:T(8,128)(2,1)S(1)} %get-tuple-element.92), channel_id=1, source_target_pairs={{0,2},{1,3},{2,0},{3,1},{4,6},{5,7},{6,4},{7,5},{8,10},{9,11},{10,... | collective-permute-start | bytes 294920 | tf_op jit(solution)/shard_map/ppermute | solution.py:462
  74.6 1.0 %collective-permute-start.32 = (bf16[16,3072]{1,0:T(8,128)(2,1)S(1)}, bf16[16,3072]{1,0:T(8,128)(2,1)S(1)}, u32[]{:S(2)}, u32[]{:S(2)}) collective-permute-start(bf16[16,3072]{1,0:T(8,128)(2,1)S(1)} %get-tuple-element.96), channel_id=1, source_target_pairs={{0,2},{1,3},{2,0},{3,1},{4,6},{5,7},{6,4},{7,5},{8,10},{9,11},{10,... | collective-permute-start | bytes 294920 | tf_op jit(solution)/shard_map/ppermute | solution.py:462
  75.5 1.5 %collective-permute-done.24.refs_2_ = bf16[16,3072]{1,0:T(8,128)(2,1)S(1)} collective-permute-done((bf16[16,3072]{1,0:T(8,128)(2,1)S(1)}, bf16[16,3072]{1,0:T(8,128)(2,1)S(1)}, u32[]{:S(2)}, u32[]{:S(2)}) %collective-permute-start.24) | collective-permute-done | bytes 98336 | tf_op jit(solution)/shard_map/ppermute | solution.py:462
  77.1 0.2 collective-permute-start.25
  77.2 1.9 %collective-permute-done.26.refs_2_ = bf16[16,3072]{1,0:T(8,128)(2,1)S(1)} collective-permute-done((bf16[16,3072]{1,0:T(8,128)(2,1)S(1)}, bf16[16,3072]{1,0:T(8,128)(2,1)S(1)}, u32[]{:S(2)}, u32[]{:S(2)}) %collective-permute-start.26) | collective-permute-done | bytes 98336 | tf_op jit(solution)/shard_map/ppermute | solution.py:462
  79.2 1.2 %collective-permute-start.27 = (bf16[8,3072]{1,0:T(8,128)(2,1)S(1)}, bf16[8,3072]{1,0:T(8,128)(2,1)S(1)}, u32[]{:S(2)}, u32[]{:S(2)}) collective-permute-start(bf16[8,3072]{1,0:T(8,128)(2,1)S(1)} %get-tuple-element.82), channel_id=1, source_target_pairs={{0,8},{4,12},{8,0},{12,4},{1,9},{5,13},{9,1},{13,5},{2,10},{6,14},... | collective-permute-start | bytes 147464 | tf_op jit(solution)/shard_map/ppermute | solution.py:462
  80.4 1.4 %collective-permute-start.28 = (bf16[8,3072]{1,0:T(8,128)(2,1)S(1)}, bf16[8,3072]{1,0:T(8,128)(2,1)S(1)}, u32[]{:S(2)}, u32[]{:S(2)}) collective-permute-start(bf16[8,3072]{1,0:T(8,128)(2,1)S(1)} %get-tuple-element.83), channel_id=1, source_target_pairs={{0,12},{4,8},{8,4},{12,0},{1,13},{5,9},{9,5},{13,1},{2,14},{6,10},... | collective-permute-start | bytes 147464 | tf_op jit(solution)/shard_map/ppermute | solution.py:462
  81.8 1.0 %collective-permute-start.31 = (bf16[8,3072]{1,0:T(8,128)(2,1)S(1)}, bf16[8,3072]{1,0:T(8,128)(2,1)S(1)}, u32[]{:S(2)}, u32[]{:S(2)}) collective-permute-start(bf16[8,3072]{1,0:T(8,128)(2,1)S(1)} %get-tuple-element.95), channel_id=1, source_target_pairs={{0,4},{4,0},{8,12},{12,8},{1,5},{5,1},{9,13},{13,9},{2,6},{6,2},{1... | collective-permute-start | bytes 147464 | tf_op jit(solution)/shard_map/ppermute | solution.py:462
  82.9 2.1 %collective-permute-start.33 = (bf16[8,3072]{1,0:T(8,128)(2,1)S(1)}, bf16[8,3072]{1,0:T(8,128)(2,1)S(1)}, u32[]{:S(2)}, u32[]{:S(2)}) collective-permute-start(bf16[8,3072]{1,0:T(8,128)(2,1)S(1)} %get-tuple-element.97), channel_id=1, source_target_pairs={{0,8},{4,12},{8,0},{12,4},{1,9},{5,13},{9,1},{13,5},{2,10},{6,14},... | collective-permute-start | bytes 147464 | tf_op jit(solution)/shard_map/ppermute | solution.py:462
  85.0 1.4 %collective-permute-start.34 = (bf16[8,3072]{1,0:T(8,128)(2,1)S(1)}, bf16[8,3072]{1,0:T(8,128)(2,1)S(1)}, u32[]{:S(2)}, u32[]{:S(2)}) collective-permute-start(bf16[8,3072]{1,0:T(8,128)(2,1)S(1)} %get-tuple-element.98), channel_id=1, source_target_pairs={{0,12},{4,8},{8,4},{12,0},{1,13},{5,9},{9,5},{13,1},{2,14},{6,10},... | collective-permute-start | bytes 147464 | tf_op jit(solution)/shard_map/ppermute | solution.py:462
  86.4 0.4 collective-permute-done.28.refs_3_
  86.8 2.7 %collective-permute-done.33.refs_6_ = bf16[8,3072]{1,0:T(8,128)(2,1)S(1)} collective-permute-done((bf16[8,3072]{1,0:T(8,128)(2,1)S(1)}, bf16[8,3072]{1,0:T(8,128)(2,1)S(1)}, u32[]{:S(2)}, u32[]{:S(2)}) %collective-permute-start.33) | collective-permute-done | bytes 49184 | tf_op jit(solution)/shard_map/ppermute | solution.py:462
  89.5 1.4 %collective-permute-done.34.refs_7_ = bf16[8,3072]{1,0:T(8,128)(2,1)S(1)} collective-permute-done((bf16[8,3072]{1,0:T(8,128)(2,1)S(1)}, bf16[8,3072]{1,0:T(8,128)(2,1)S(1)}, u32[]{:S(2)}, u32[]{:S(2)}) %collective-permute-start.34) | collective-permute-done | bytes 49184 | tf_op jit(solution)/shard_map/ppermute | solution.py:462
  90.9 0.9 %mix.1 = bf16[24,3072]{1,0:T(8,128)(2,1)} custom-call(f32[24,3072]{1,0:T(8,128)S(1)} %get-tuple-element.64.residual_ref, f32[24,64]{1,0:T(8,128)S(1)} %get-tuple-element.65.map_ref, bf16[8,3072]{1,0:T(8,128)(2,1)S(1)} %get-tuple-element.79.refs_0_, bf16[8,3072]{1,0:T(8,128)(2,1)S(1)} %collective-permute-done.25.refs_1_, ...), custom_call_target="tpu_custom_call" | custom-call | tf_op jit(solution)/shard_map/mix/pallas_call | solution.py:701
  (33 shorter events, 0.3 us)
Async XLA Ops:
  1.1 12.6 %collective-permute-start = (bf16[256,256]{1,0:T(8,128)(2,1)S(1)}, bf16[256,256]{1,0:T(8,128)(2,1)S(1)}, u32[]{:S(2)}, u32[]{:S(2)}) collective-permute-start(bf16[256,256]{1,0:T(8,128)(2,1)S(1)} %get-tuple-element.53), channel_id=1, source_target_pairs={{0,1},{1,0},{2,3},{3,2},{4,5},{5,4},{6,7},{7,6},{8,9},{9,8},{10,11... | collective-permute-start | bytes 393224 | tf_op jit(solution)/shard_map/ppermute | solution.py:530
  1.7 12.1 %collective-permute-start.1 = (bf16[256,256]{1,0:T(8,128)(2,1)S(1)}, bf16[256,256]{1,0:T(8,128)(2,1)S(1)}, u32[]{:S(2)}, u32[]{:S(2)}) collective-permute-start(bf16[256,256]{1,0:T(8,128)(2,1)S(1)} %get-tuple-element.54), channel_id=1, source_target_pairs={{0,2},{1,3},{2,0},{3,1},{4,6},{5,7},{6,4},{7,5},{8,10},{9,11},{10,... | collective-permute-start | bytes 393224 | tf_op jit(solution)/shard_map/ppermute | solution.py:530
  4.3 9.5 %collective-permute-start.2 = (bf16[256,256]{1,0:T(8,128)(2,1)S(1)}, bf16[256,256]{1,0:T(8,128)(2,1)S(1)}, u32[]{:S(2)}, u32[]{:S(2)}) collective-permute-start(bf16[256,256]{1,0:T(8,128)(2,1)S(1)} %get-tuple-element.55), channel_id=1, source_target_pairs={{0,3},{1,2},{2,1},{3,0},{4,7},{5,6},{6,5},{7,4},{8,11},{9,10},{10,... | collective-permute-start | bytes 393224 | tf_op jit(solution)/shard_map/ppermute | solution.py:530
  8.4 2.2 %collective-permute-start.3 = (bf16[48,128]{1,0:T(8,128)(2,1)S(1)}, bf16[48,128]{1,0:T(8,128)(2,1)S(1)}, u32[]{:S(2)}, u32[]{:S(2)}) collective-permute-start(bf16[48,128]{1,0:T(8,128)(2,1)S(1)} %get-tuple-element.57), channel_id=1, source_target_pairs={{0,1},{1,0},{2,3},{3,2},{4,5},{5,4},{6,7},{7,6},{8,9},{9,8},{10,11... | collective-permute-start | bytes 36872 | tf_op jit(solution)/shard_map/ppermute | solution.py:551
  8.6 3.7 %collective-permute-start.4 = (bf16[48,128]{1,0:T(8,128)(2,1)S(1)}, bf16[48,128]{1,0:T(8,128)(2,1)S(1)}, u32[]{:S(2)}, u32[]{:S(2)}) collective-permute-start(bf16[48,128]{1,0:T(8,128)(2,1)S(1)} %get-tuple-element.58), channel_id=1, source_target_pairs={{0,2},{1,3},{2,0},{3,1},{4,6},{5,7},{6,4},{7,5},{8,10},{9,11},{10,... | collective-permute-start | bytes 36872 | tf_op jit(solution)/shard_map/ppermute | solution.py:551
  10.6 3.2 %collective-permute-start.5 = (bf16[48,128]{1,0:T(8,128)(2,1)S(1)}, bf16[48,128]{1,0:T(8,128)(2,1)S(1)}, u32[]{:S(2)}, u32[]{:S(2)}) collective-permute-start(bf16[48,128]{1,0:T(8,128)(2,1)S(1)} %get-tuple-element.59), channel_id=1, source_target_pairs={{0,3},{1,2},{2,1},{3,0},{4,7},{5,6},{6,5},{7,4},{8,11},{9,10},{10,... | collective-permute-start | bytes 36872 | tf_op jit(solution)/shard_map/ppermute | solution.py:551
  18.4 1.6 %collective-permute-start.6 = (bf16[48,3072]{1,0:T(8,128)(2,1)S(1)}, bf16[48,3072]{1,0:T(8,128)(2,1)S(1)}, u32[]{:S(2)}, u32[]{:S(2)}) collective-permute-start(bf16[48,3072]{1,0:T(8,128)(2,1)S(1)} %get-tuple-element.62), channel_id=1, source_target_pairs={{0,1},{1,0},{2,3},{3,2},{4,5},{5,4},{6,7},{7,6},{8,9},{9,8},{10,11... | collective-permute-start | bytes 884744 | tf_op jit(solution)/shard_map/ppermute | solution.py:462
  20.1 6.0 %copy-start = (bf16[24,3072]{1,0:T(8,128)(2,1)S(1)}, bf16[24,3072]{1,0:T(8,128)(2,1)}, u32[]{:S(2)}) copy-start(bf16[24,3072]{1,0:T(8,128)(2,1)} %refs_3_.1) | copy-start | bytes 442372
  20.1 6.0 %copy-start.1 = (bf16[3072,8]{0,1:T(8,128)(2,1)S(1)}, bf16[3072,8]{0,1:T(8,128)(2,1)}, u32[]{:S(2)}) copy-start(bf16[3072,8]{0,1:T(8,128)(2,1)} %param.23) | copy-start | bytes 147460
  20.1 6.0 %copy-start.2 = (f32[3072]{0:T(1024)S(1)}, f32[3072]{0:T(1024)}, u32[]{:S(2)}) copy-start(f32[3072]{0:T(1024)} %param.22) | copy-start | bytes 36868
  20.1 6.0 %copy-start.3 = (s32[24,2]{0,1:T(2,128)S(1)}, s32[24,2]{0,1:T(2,128)}, u32[]{:S(2)}) copy-start(s32[24,2]{0,1:T(2,128)} %param.24) | copy-start | bytes 580
  20.1 6.0 %collective-permute-start.7 = (bf16[24,3072]{1,0:T(8,128)(2,1)S(1)}, bf16[24,3072]{1,0:T(8,128)(2,1)S(1)}, u32[]{:S(2)}, u32[]{:S(2)}) collective-permute-start(bf16[24,3072]{1,0:T(8,128)(2,1)S(1)} %shard_map.139._), channel_id=1, source_target_pairs={{0,2},{1,3},{2,0},{3,1},{4,6},{5,7},{6,4},{7,5},{8,10},{9,11},{10,... | collective-permute-start | bytes 442376 | tf_op jit(solution)/shard_map/ppermute | solution.py:462
  26.6 5.7 %collective-permute-start.8 = (bf16[16,3072]{1,0:T(8,128)(2,1)S(1)}, bf16[16,3072]{1,0:T(8,128)(2,1)S(1)}, u32[]{:S(2)}, u32[]{:S(2)}) collective-permute-start(bf16[16,3072]{1,0:T(8,128)(2,1)S(1)} %get-tuple-element.67), channel_id=1, source_target_pairs={{0,4},{4,0},{8,12},{12,8},{1,5},{5,1},{9,13},{13,9},{2,6},{6,2},{1... | collective-permute-start | bytes 294920 | tf_op jit(solution)/shard_map/ppermute | solution.py:462
  28.3 10.1 %collective-permute-start.9 = (bf16[16,3072]{1,0:T(8,128)(2,1)S(1)}, bf16[16,3072]{1,0:T(8,128)(2,1)S(1)}, u32[]{:S(2)}, u32[]{:S(2)}) collective-permute-start(bf16[16,3072]{1,0:T(8,128)(2,1)S(1)} %get-tuple-element.68), channel_id=1, source_target_pairs={{0,8},{4,12},{8,0},{12,4},{1,9},{5,13},{9,1},{13,5},{2,10},{6,14},... | collective-permute-start | bytes 294920 | tf_op jit(solution)/shard_map/ppermute | solution.py:462
  30.9 8.6 %collective-permute-start.10 = (bf16[16,3072]{1,0:T(8,128)(2,1)S(1)}, bf16[16,3072]{1,0:T(8,128)(2,1)S(1)}, u32[]{:S(2)}, u32[]{:S(2)}) collective-permute-start(bf16[16,3072]{1,0:T(8,128)(2,1)S(1)} %get-tuple-element.69), channel_id=1, source_target_pairs={{0,12},{4,8},{8,4},{12,0},{1,13},{5,9},{9,5},{13,1},{2,14},{6,10},... | collective-permute-start | bytes 294920 | tf_op jit(solution)/shard_map/ppermute | solution.py:462
  31.1 8.4 %collective-permute-start.15 = (bf16[16,3072]{1,0:T(8,128)(2,1)S(1)}, bf16[16,3072]{1,0:T(8,128)(2,1)S(1)}, u32[]{:S(2)}, u32[]{:S(2)}) collective-permute-start(bf16[16,3072]{1,0:T(8,128)(2,1)S(1)} %get-tuple-element.66._.refs_0_), channel_id=1, source_target_pairs={{0,1},{1,0},{2,3},{3,2},{4,5},{5,4},{6,7},{7,6},{8,9},{9,8},{10,11... | collective-permute-start | bytes 294920 | tf_op jit(solution)/shard_map/ppermute | solution.py:462
  31.1 9.4 %collective-permute-start.11 = (bf16[16,3072]{1,0:T(8,128)(2,1)S(1)}, bf16[16,3072]{1,0:T(8,128)(2,1)S(1)}, u32[]{:S(2)}, u32[]{:S(2)}) collective-permute-start(bf16[16,3072]{1,0:T(8,128)(2,1)S(1)} %get-tuple-element.66._.refs_0_), channel_id=1, source_target_pairs={{0,2},{1,3},{2,0},{3,1},{4,6},{5,7},{6,4},{7,5},{8,10},{9,11},{10,... | collective-permute-start | bytes 294920 | tf_op jit(solution)/shard_map/ppermute | solution.py:462
  32.3 9.3 %collective-permute-start.16 = (bf16[16,3072]{1,0:T(8,128)(2,1)S(1)}, bf16[16,3072]{1,0:T(8,128)(2,1)S(1)}, u32[]{:S(2)}, u32[]{:S(2)}) collective-permute-start(bf16[16,3072]{1,0:T(8,128)(2,1)S(1)} %collective-permute-done.8.refs_1_), channel_id=1, source_target_pairs={{0,1},{1,0},{2,3},{3,2},{4,5},{5,4},{6,7},{7,6},{8,9},{9,8},{10,11... | collective-permute-start | bytes 294920 | tf_op jit(solution)/shard_map/ppermute | solution.py:462
  38.4 5.1 %collective-permute-start.12 = (bf16[16,3072]{1,0:T(8,128)(2,1)S(1)}, bf16[16,3072]{1,0:T(8,128)(2,1)S(1)}, u32[]{:S(2)}, u32[]{:S(2)}) collective-permute-start(bf16[16,3072]{1,0:T(8,128)(2,1)S(1)} %collective-permute-done.8.refs_1_), channel_id=1, source_target_pairs={{0,2},{1,3},{2,0},{3,1},{4,6},{5,7},{6,4},{7,5},{8,10},{9,11},{10,... | collective-permute-start | bytes 294920 | tf_op jit(solution)/shard_map/ppermute | solution.py:462
  39.5 4.0 %collective-permute-start.17 = (bf16[16,3072]{1,0:T(8,128)(2,1)S(1)}, bf16[16,3072]{1,0:T(8,128)(2,1)S(1)}, u32[]{:S(2)}, u32[]{:S(2)}) collective-permute-start(bf16[16,3072]{1,0:T(8,128)(2,1)S(1)} %collective-permute-done.9.refs_2_), channel_id=1, source_target_pairs={{0,1},{1,0},{2,3},{3,2},{4,5},{5,4},{6,7},{7,6},{8,9},{9,8},{10,11... | collective-permute-start | bytes 294920 | tf_op jit(solution)/shard_map/ppermute | solution.py:462
  39.5 6.1 %collective-permute-start.13 = (bf16[16,3072]{1,0:T(8,128)(2,1)S(1)}, bf16[16,3072]{1,0:T(8,128)(2,1)S(1)}, u32[]{:S(2)}, u32[]{:S(2)}) collective-permute-start(bf16[16,3072]{1,0:T(8,128)(2,1)S(1)} %collective-permute-done.9.refs_2_), channel_id=1, source_target_pairs={{0,2},{1,3},{2,0},{3,1},{4,6},{5,7},{6,4},{7,5},{8,10},{9,11},{10,... | collective-permute-start | bytes 294920 | tf_op jit(solution)/shard_map/ppermute | solution.py:462
  40.5 6.7 %collective-permute-start.14 = (bf16[16,3072]{1,0:T(8,128)(2,1)S(1)}, bf16[16,3072]{1,0:T(8,128)(2,1)S(1)}, u32[]{:S(2)}, u32[]{:S(2)}) collective-permute-start(bf16[16,3072]{1,0:T(8,128)(2,1)S(1)} %collective-permute-done.10.refs_3_), channel_id=1, source_target_pairs={{0,2},{1,3},{2,0},{3,1},{4,6},{5,7},{6,4},{7,5},{8,10},{9,11},{10,... | collective-permute-start | bytes 294920 | tf_op jit(solution)/shard_map/ppermute | solution.py:462
  41.6 11.9 %collective-permute-start.18 = (bf16[16,3072]{1,0:T(8,128)(2,1)S(1)}, bf16[16,3072]{1,0:T(8,128)(2,1)S(1)}, u32[]{:S(2)}, u32[]{:S(2)}) collective-permute-start(bf16[16,3072]{1,0:T(8,128)(2,1)S(1)} %collective-permute-done.10.refs_3_), channel_id=1, source_target_pairs={{0,1},{1,0},{2,3},{3,2},{4,5},{5,4},{6,7},{7,6},{8,9},{9,8},{10,11... | collective-permute-start | bytes 294920 | tf_op jit(solution)/shard_map/ppermute | solution.py:462
  43.5 10.0 %collective-permute-start.19 = (bf16[16,3072]{1,0:T(8,128)(2,1)S(1)}, bf16[16,3072]{1,0:T(8,128)(2,1)S(1)}, u32[]{:S(2)}, u32[]{:S(2)}) collective-permute-start(bf16[16,3072]{1,0:T(8,128)(2,1)S(1)} %collective-permute-done.11.refs_4_), channel_id=1, source_target_pairs={{0,1},{1,0},{2,3},{3,2},{4,5},{5,4},{6,7},{7,6},{8,9},{9,8},{10,11... | collective-permute-start | bytes 294920 | tf_op jit(solution)/shard_map/ppermute | solution.py:462
  43.5 10.0 %collective-permute-start.20 = (bf16[16,3072]{1,0:T(8,128)(2,1)S(1)}, bf16[16,3072]{1,0:T(8,128)(2,1)S(1)}, u32[]{:S(2)}, u32[]{:S(2)}) collective-permute-start(bf16[16,3072]{1,0:T(8,128)(2,1)S(1)} %collective-permute-done.12.refs_5_), channel_id=1, source_target_pairs={{0,1},{1,0},{2,3},{3,2},{4,5},{5,4},{6,7},{7,6},{8,9},{9,8},{10,11... | collective-permute-start | bytes 294920 | tf_op jit(solution)/shard_map/ppermute | solution.py:462
  45.6 7.9 %collective-permute-start.21 = (bf16[16,3072]{1,0:T(8,128)(2,1)S(1)}, bf16[16,3072]{1,0:T(8,128)(2,1)S(1)}, u32[]{:S(2)}, u32[]{:S(2)}) collective-permute-start(bf16[16,3072]{1,0:T(8,128)(2,1)S(1)} %collective-permute-done.13.refs_6_), channel_id=1, source_target_pairs={{0,1},{1,0},{2,3},{3,2},{4,5},{5,4},{6,7},{7,6},{8,9},{9,8},{10,11... | collective-permute-start | bytes 294920 | tf_op jit(solution)/shard_map/ppermute | solution.py:462
  47.3 6.2 %collective-permute-start.22 = (bf16[16,3072]{1,0:T(8,128)(2,1)S(1)}, bf16[16,3072]{1,0:T(8,128)(2,1)S(1)}, u32[]{:S(2)}, u32[]{:S(2)}) collective-permute-start(bf16[16,3072]{1,0:T(8,128)(2,1)S(1)} %collective-permute-done.14.refs_7_), channel_id=1, source_target_pairs={{0,1},{1,0},{2,3},{3,2},{4,5},{5,4},{6,7},{7,6},{8,9},{9,8},{10,11... | collective-permute-start | bytes 294920 | tf_op jit(solution)/shard_map/ppermute | solution.py:462
  60.7 6.3 %collective-permute-start.23 = (bf16[64,3072]{1,0:T(8,128)(2,1)S(1)}, bf16[64,3072]{1,0:T(8,128)(2,1)S(1)}, u32[]{:S(2)}, u32[]{:S(2)}) collective-permute-start(bf16[64,3072]{1,0:T(8,128)(2,1)S(1)} %get-tuple-element.77), channel_id=1, source_target_pairs={{0,1},{1,0},{2,3},{3,2},{4,5},{5,4},{6,7},{7,6},{8,9},{9,8},{10,11... | collective-permute-start | bytes 1179656 | tf_op jit(solution)/shard_map/ppermute | solution.py:462
  71.2 2.2 %collective-permute-start.29 = (bf16[64,3072]{1,0:T(8,128)(2,1)S(1)}, bf16[64,3072]{1,0:T(8,128)(2,1)S(1)}, u32[]{:S(2)}, u32[]{:S(2)}) collective-permute-start(bf16[64,3072]{1,0:T(8,128)(2,1)S(1)} %get-tuple-element.91), channel_id=1, source_target_pairs={{0,1},{1,0},{2,3},{3,2},{4,5},{5,4},{6,7},{7,6},{8,9},{9,8},{10,11... | collective-permute-start | bytes 1179656 | tf_op jit(solution)/shard_map/ppermute | solution.py:462
  71.3 5.7 %collective-permute-start.24 = (bf16[16,3072]{1,0:T(8,128)(2,1)S(1)}, bf16[16,3072]{1,0:T(8,128)(2,1)S(1)}, u32[]{:S(2)}, u32[]{:S(2)}) collective-permute-start(bf16[16,3072]{1,0:T(8,128)(2,1)S(1)} %get-tuple-element.78), channel_id=1, source_target_pairs={{0,2},{1,3},{2,0},{3,1},{4,6},{5,7},{6,4},{7,5},{8,10},{9,11},{10,... | collective-permute-start | bytes 294920 | tf_op jit(solution)/shard_map/ppermute | solution.py:462
  72.4 6.7 %collective-permute-start.26 = (bf16[16,3072]{1,0:T(8,128)(2,1)S(1)}, bf16[16,3072]{1,0:T(8,128)(2,1)S(1)}, u32[]{:S(2)}, u32[]{:S(2)}) collective-permute-start(bf16[16,3072]{1,0:T(8,128)(2,1)S(1)} %get-tuple-element.81.refs_2_), channel_id=1, source_target_pairs={{0,2},{1,3},{2,0},{3,1},{4,6},{5,7},{6,4},{7,5},{8,10},{9,11},{10,... | collective-permute-start | bytes 294920 | tf_op jit(solution)/shard_map/ppermute | solution.py:462
  73.4 8.4 %collective-permute-start.30 = (bf16[16,3072]{1,0:T(8,128)(2,1)S(1)}, bf16[16,3072]{1,0:T(8,128)(2,1)S(1)}, u32[]{:S(2)}, u32[]{:S(2)}) collective-permute-start(bf16[16,3072]{1,0:T(8,128)(2,1)S(1)} %get-tuple-element.92), channel_id=1, source_target_pairs={{0,2},{1,3},{2,0},{3,1},{4,6},{5,7},{6,4},{7,5},{8,10},{9,11},{10,... | collective-permute-start | bytes 294920 | tf_op jit(solution)/shard_map/ppermute | solution.py:462
  74.6 8.3 %collective-permute-start.32 = (bf16[16,3072]{1,0:T(8,128)(2,1)S(1)}, bf16[16,3072]{1,0:T(8,128)(2,1)S(1)}, u32[]{:S(2)}, u32[]{:S(2)}) collective-permute-start(bf16[16,3072]{1,0:T(8,128)(2,1)S(1)} %get-tuple-element.96), channel_id=1, source_target_pairs={{0,2},{1,3},{2,0},{3,1},{4,6},{5,7},{6,4},{7,5},{8,10},{9,11},{10,... | collective-permute-start | bytes 294920 | tf_op jit(solution)/shard_map/ppermute | solution.py:462
  77.1 7.9 %collective-permute-start.25 = (bf16[8,3072]{1,0:T(8,128)(2,1)S(1)}, bf16[8,3072]{1,0:T(8,128)(2,1)S(1)}, u32[]{:S(2)}, u32[]{:S(2)}) collective-permute-start(bf16[8,3072]{1,0:T(8,128)(2,1)S(1)} %get-tuple-element.80), channel_id=1, source_target_pairs={{0,4},{4,0},{8,12},{12,8},{1,5},{5,1},{9,13},{13,9},{2,6},{6,2},{1... | collective-permute-start | bytes 147464 | tf_op jit(solution)/shard_map/ppermute | solution.py:462
  79.2 7.2 %collective-permute-start.27 = (bf16[8,3072]{1,0:T(8,128)(2,1)S(1)}, bf16[8,3072]{1,0:T(8,128)(2,1)S(1)}, u32[]{:S(2)}, u32[]{:S(2)}) collective-permute-start(bf16[8,3072]{1,0:T(8,128)(2,1)S(1)} %get-tuple-element.82), channel_id=1, source_target_pairs={{0,8},{4,12},{8,0},{12,4},{1,9},{5,13},{9,1},{13,5},{2,10},{6,14},... | collective-permute-start | bytes 147464 | tf_op jit(solution)/shard_map/ppermute | solution.py:462
  80.4 6.4 %collective-permute-start.28 = (bf16[8,3072]{1,0:T(8,128)(2,1)S(1)}, bf16[8,3072]{1,0:T(8,128)(2,1)S(1)}, u32[]{:S(2)}, u32[]{:S(2)}) collective-permute-start(bf16[8,3072]{1,0:T(8,128)(2,1)S(1)} %get-tuple-element.83), channel_id=1, source_target_pairs={{0,12},{4,8},{8,4},{12,0},{1,13},{5,9},{9,5},{13,1},{2,14},{6,10},... | collective-permute-start | bytes 147464 | tf_op jit(solution)/shard_map/ppermute | solution.py:462
  81.8 5.0 %collective-permute-start.31 = (bf16[8,3072]{1,0:T(8,128)(2,1)S(1)}, bf16[8,3072]{1,0:T(8,128)(2,1)S(1)}, u32[]{:S(2)}, u32[]{:S(2)}) collective-permute-start(bf16[8,3072]{1,0:T(8,128)(2,1)S(1)} %get-tuple-element.95), channel_id=1, source_target_pairs={{0,4},{4,0},{8,12},{12,8},{1,5},{5,1},{9,13},{13,9},{2,6},{6,2},{1... | collective-permute-start | bytes 147464 | tf_op jit(solution)/shard_map/ppermute | solution.py:462
  82.9 6.6 %collective-permute-start.33 = (bf16[8,3072]{1,0:T(8,128)(2,1)S(1)}, bf16[8,3072]{1,0:T(8,128)(2,1)S(1)}, u32[]{:S(2)}, u32[]{:S(2)}) collective-permute-start(bf16[8,3072]{1,0:T(8,128)(2,1)S(1)} %get-tuple-element.97), channel_id=1, source_target_pairs={{0,8},{4,12},{8,0},{12,4},{1,9},{5,13},{9,1},{13,5},{2,10},{6,14},... | collective-permute-start | bytes 147464 | tf_op jit(solution)/shard_map/ppermute | solution.py:462
  85.0 5.9 %collective-permute-start.34 = (bf16[8,3072]{1,0:T(8,128)(2,1)S(1)}, bf16[8,3072]{1,0:T(8,128)(2,1)S(1)}, u32[]{:S(2)}, u32[]{:S(2)}) collective-permute-start(bf16[8,3072]{1,0:T(8,128)(2,1)S(1)} %get-tuple-element.98), channel_id=1, source_target_pairs={{0,12},{4,8},{8,4},{12,0},{1,13},{5,9},{9,5},{13,1},{2,14},{6,10},... | collective-permute-start | bytes 147464 | tf_op jit(solution)/shard_map/ppermute | solution.py:462
